TPU v7x, 128 devices: a whole 4x4x4 slice. The times are simulated.
128 devices in a mesh: node: 16 (over z, x), local: 8 (over y, core).
Axes of the slice: x: 4, y: 4, z: 4, core: 2. Of those that a mesh axis runs over, the one named last changes fastest.
Arguments:
- tokens: bfloat16 [65536, 2048], P(('node', 'local')), may hold values from -64 to 64, as said below
- d_out: bfloat16 [65536, 1024], P(('node', 'local')), may hold values from -6 to 6
- w_query: bfloat16 [2048, 1536], P('local'), may hold values from -0.125 to 0.125
- w_down: bfloat16 [2048, 576], P('local'), may hold values from -0.125 to 0.125
- w_up: bfloat16 [512, 2048], P('local'), may hold values from -0.25 to 0.25
- latent_gain: bfloat16 [512], P('local'), may hold values from 0.5 to 1.5
Outputs:
- grad_query: float32 [2048, 1536], P(('node', 'local'))
- grad_down: float32 [2048, 576], P(('node', 'local'))
- grad_up: float32 [512, 2048], P(('node', 'local'))
- grad_gain: float32 [512], P(('node', 'local'))
- grad_tokens: bfloat16 [65536, 2048], P(('node', 'local'))
Inputs may be any that keep to these rules, and one draw needn't show every extreme that they name: `tokens`: real-valued rows of the layer's normed input.
All inputs are finite; a program needn't handle non-finite values.
Results may differ from a plain program's by a relative error of at most 0.014.
The roundings to bfloat16 on the way count: a program that leaves them out, or rounds other values in their place, can miss the bound.
Values may be sent and summed in bfloat16 or wider, within the bound.
A program may use at most 128 MiB of HBM per device.

v0:
```python
import math

import jax
import jax.numpy as jnp
from jax import lax
from jax.sharding import Mesh
from jax.sharding import PartitionSpec as P

H = 8
DN = 128
DR = 64
DV = 128
KVL = 512
NPARAM = 5374464
LOCAL = ("local_0", "local_1")
NODE = ("node_0", "node_1")
NODE_LOCAL = ("node_0", "node_1", "local_0", "local_1")


EPSILON = 1e-06
ROPE_BASE = 10000.0


def sent_together(arrays, axis, dim, along):
    columns = [a.reshape(*a.shape[:along], -1) for a in arrays]
    both = jnp.concatenate(columns, axis=along)
    filled, at, gathered = (lax.all_gather(both, axis, axis=dim, tiled=True), 0, [])
    for a, column in zip(arrays, columns):
        piece = filled[..., at : at + column.shape[along]]
        gathered.append(piece.reshape(*piece.shape[:along], *a.shape[along:]))
        at += column.shape[along]
    return tuple(gathered)


def sent_together_2(arrays, axis, dim, along):
    widths = [a.shape[along] for a in arrays]
    both = jnp.concatenate(arrays, axis=along)
    filled = lax.all_gather(both, axis, axis=dim, tiled=True)
    return tuple(jnp.split(filled, [sum(widths[:k]) for k in range(1, len(widths))], axis=along))


def cut_along(shard, dim, size):
    before, after = (shard.shape[:dim], shard.shape[dim + 1 :])
    return jnp.moveaxis(shard.reshape(*before, size, -1, *after), dim, 0)


def sum_at_owner(shard, axis, dim):
    size = lax.axis_size(axis)
    pieces = lax.all_to_all(cut_along(shard, dim, size), axis, 0, 0, tiled=True)
    return jnp.sum(pieces, axis=0)


def sent_together_3(arrays, axis, dim, along):
    columns = [a.reshape(*a.shape[:along], -1) for a in arrays]
    both = jnp.concatenate(columns, axis=along)
    filled, at, gathered = (lax.psum_scatter(both, axis, scatter_dimension=dim, tiled=True), 0, [])
    for a, column in zip(arrays, columns):
        piece = filled[..., at : at + column.shape[along]]
        gathered.append(piece.reshape(*piece.shape[:along], *a.shape[along:]))
        at += column.shape[along]
    return tuple(gathered)


def in_one_piece(arrays, axis, dim, along):
    columns = [a.reshape(*a.shape[:along], -1) for a in arrays]
    both = jnp.concatenate(columns, axis=along)
    filled, at, gathered = (sum_at_owner(both, axis, dim), 0, [])
    for a, column in zip(arrays, columns):
        piece = filled[..., at : at + column.shape[along]]
        gathered.append(piece.reshape(*piece.shape[:along], *a.shape[along:]))
        at += column.shape[along]
    return tuple(gathered)


def one_axis_at_a_time(shard, axes):
    for axis in axes:
        shard = lax.psum(shard, axis)
    return shard


def rope_tables(length, width):
    position = jnp.arange(length, dtype=jnp.float32)[:, None]
    freq = ROPE_BASE ** (-jnp.arange(width // 2, dtype=jnp.float32) * 2.0 / width)
    angle = position * freq[None, :]
    return (jnp.cos(angle), jnp.sin(angle))


def rotate(values, cosine, sine):
    half = values.shape[-1] // 2
    first = values[..., :half]
    second = values[..., half:]
    return jnp.concatenate([first * cosine - second * sine, second * cosine + first * sine], -1)


def transposed_product(left, right):
    return lax.dot_general(
        left, right, (((1,), (1,)), ((), ())), preferred_element_type=jnp.float32
    )


def local_backward(query32, down32, d_o, w_up, gain):
    length = query32.shape[0]
    cosine, sine = rope_tables(length, DR)
    query = query32.astype(jnp.bfloat16).reshape(length, H, DN + DR)
    latent = down32[:, :KVL]
    rope_raw = down32[:, KVL:]
    inv_rms = lax.rsqrt(jnp.mean(latent * latent, axis=-1, keepdims=True) + EPSILON)
    unit = latent * inv_rms
    gain32 = gain.astype(jnp.float32)
    normed = (unit * gain32).astype(jnp.bfloat16)
    keyval = jnp.dot(normed, w_up, preferred_element_type=jnp.float32).astype(jnp.bfloat16)
    keyval = keyval.reshape(length, H, DN + DV)
    key_nope = keyval[..., :DN]
    values = keyval[..., DN:]
    query_rope = rotate(
        query[..., DN:].astype(jnp.float32), cosine[:, None, :], sine[:, None, :]
    ).astype(jnp.bfloat16)
    key_rope = rotate(rope_raw, cosine, sine).astype(jnp.bfloat16)
    query_full = jnp.concatenate([query[..., :DN], query_rope], -1)
    key_full = jnp.concatenate(
        [key_nope, jnp.broadcast_to(key_rope[:, None, :], (length, H, DR))], -1
    )
    scale = 1.0 / math.sqrt(DN + DR)
    scores = (
        jnp.einsum("qhd,khd->hqk", query_full, key_full, preferred_element_type=jnp.float32) * scale
    )
    causal = jnp.arange(length)[:, None] >= jnp.arange(length)[None, :]
    scores = jnp.where(causal[None], scores, -1e30)
    highest = jnp.max(scores, axis=-1, keepdims=True)
    weights = jnp.exp(scores - highest)
    probs = weights / jnp.sum(weights, axis=-1, keepdims=True)
    probs_b = probs.astype(jnp.bfloat16)
    grad_out = d_o.reshape(length, H, DV)
    dprobs = jnp.einsum("qhd,khd->hqk", grad_out, values, preferred_element_type=jnp.float32)
    delta = jnp.sum(probs * dprobs, axis=-1, keepdims=True)
    dscores = (probs * (dprobs - delta) * scale).astype(jnp.bfloat16)
    dquery = jnp.einsum("hqk,khd->qhd", dscores, key_full, preferred_element_type=jnp.float32)
    dkey = jnp.einsum("hqk,qhd->khd", dscores, query_full, preferred_element_type=jnp.float32)
    dvalues = jnp.einsum("hqk,qhd->khd", probs_b, grad_out, preferred_element_type=jnp.float32)
    dquery_rope = rotate(dquery[..., DN:], cosine[:, None, :], -sine[:, None, :])
    query_grad = (
        jnp.concatenate([dquery[..., :DN], dquery_rope], -1)
        .reshape(length, H * (DN + DR))
        .astype(jnp.bfloat16)
    )
    rope_grad = rotate(jnp.sum(dkey[..., DN:], axis=1), cosine, -sine)
    keyval_grad = (
        jnp.concatenate([dkey[..., :DN], dvalues], -1)
        .reshape(length, H * (DN + DV))
        .astype(jnp.bfloat16)
    )
    normed_grad = transposed_product(keyval_grad, w_up)
    gain_term = jnp.sum(normed_grad * unit, axis=0)
    scaled = normed_grad * gain32
    latent_grad = inv_rms * (scaled - unit * jnp.mean(scaled * unit, axis=-1, keepdims=True))
    down_grad = jnp.concatenate([latent_grad, rope_grad], -1).astype(jnp.bfloat16)
    return (query_grad, down_grad, normed, keyval_grad, gain_term)


def per_device(tokens, d_out, w_query, w_down, w_up, latent_gain):
    width_query = w_query.shape[1]
    up_full, gain_full = sent_together((w_up, latent_gain), LOCAL, 0, 1)
    query_full_w, down_full_w = sent_together_2((w_query, w_down), LOCAL, 0, 1)
    query32 = jnp.dot(tokens, query_full_w, preferred_element_type=jnp.float32)
    down32 = jnp.dot(tokens, down_full_w, preferred_element_type=jnp.float32)
    query_grad, down_grad, normed, keyval_grad, gain_term = local_backward(
        query32, down32, d_out, up_full, gain_full
    )
    token_grad = transposed_product(query_grad, query_full_w) + transposed_product(
        down_grad, down_full_w
    )
    joined = jnp.concatenate([query_grad, down_grad], 1)
    up_term = lax.dot_general(
        normed, keyval_grad, (((0,), (0,)), ((), ())), preferred_element_type=jnp.float32
    )
    node_block = lax.psum_scatter(
        lax.dot_general(
            tokens, joined, (((0,), (0,)), ((), ())), preferred_element_type=jnp.float32
        ),
        NODE,
        scatter_dimension=0,
        tiled=True,
    )
    input_sum = sum_at_owner(node_block, LOCAL, 0)
    node_part = sent_together_3((up_term, gain_term), NODE, 0, 1)
    up_sum, gain_sum = in_one_piece((node_part[0], node_part[1]), LOCAL, 0, 1)
    squares = (
        jnp.sum(input_sum * input_sum) + jnp.sum(up_sum * up_sum) + jnp.sum(gain_sum * gain_sum)
    )
    total = one_axis_at_a_time(squares, NODE_LOCAL)
    clip = jnp.minimum(1.0, lax.rsqrt(total / NPARAM + 1e-06))
    return (
        input_sum[:, :width_query] * clip,
        input_sum[:, width_query:] * clip,
        up_sum * clip,
        gain_sum * clip,
        token_grad.astype(jnp.bfloat16),
    )


def solution(mesh):
    split = Mesh(mesh.devices.reshape(4, 4, 4, 2), ("node_0", "node_1", "local_0", "local_1"))
    return jax.shard_map(
        per_device,
        mesh=split,
        in_specs=(
            P(NODE_LOCAL, None),
            P(NODE_LOCAL, None),
            P(LOCAL, None),
            P(LOCAL, None),
            P(LOCAL, None),
            P(LOCAL),
        ),
        out_specs=(
            P(NODE_LOCAL, None),
            P(NODE_LOCAL, None),
            P(NODE_LOCAL, None),
            P(NODE_LOCAL),
            P(NODE_LOCAL, None),
        ),
        check_vma=False,
    )
```

profile of v0, /device:TPU:1, one launch (start us, length us, event | category | flops | bytes accessed | tf_op | source)
XLA Modules:
  0.0 439.6 jit_solution(10245511770562962368)
XLA Ops:
  7.2 0.9 copy.21
  8.2 1.7 pad_maximum_fusion.10
  9.9 1.2 copy.20
  11.1 2.2 pad_maximum_fusion.7
  13.4 1.4 copy.36
  14.8 0.8 iota_compare_fusion
  15.6 23.5 %all-gather.5.cloned.1.call-done = bf16[512,2049]{1,0:T(8,128)(2,1)} async-done(((bf16[64,2049]{1,0:T(8,128)(2,1)}), bf16[512,2049]{1,0:T(8,128)(2,1)}) %all-gather.5.cloned.1.call-update) | async-done | bytes 2098192 | tf_op jit(solution)/shard_map/all_gather | solution.py:27
  39.1 1.0 convert_reduce_fusion
  40.1 53.6 %all-gather.3.cloned.1.call-done = bf16[2048,2112]{1,0:T(8,128)(2,1)} async-done(((bf16[256,2112]{1,0:T(8,128)(2,1)}), bf16[2048,2112]{1,0:T(8,128)(2,1)}) %all-gather.3.cloned.1.call-update) | async-done | bytes 8650768 | tf_op jit(solution)/shard_map/all_gather | solution.py:38
  93.7 6.4 %fusion.18 = bf16[1536,512]{1,0:T(8,128)(2,1)S(1)} fusion(bf16[512,2048]{1,0:T(8,128)(2,1)S(1)} %copy-done, bf16[2048,2112]{1,0:T(8,128)(2,1)} %all-gather.3.cloned.1.call-done), kind=kOutput, calls=%fused_computation.26 | convolution fusion | flops 3222011904 | bytes 9961472 | tf_op jit(solution)/shard_map/dot_general | solution.py:164
  100.0 1.1 slice_convert_fusion.2
  101.2 1.1 slice.105
  102.3 3.6 fusion.39
  105.9 0.1 multiply_reduce_fusion.2
  106.0 1.0 fusion.55
  107.0 1.4 convolution_convert_fusion
  108.4 0.7 copy.37
  109.1 1.5 fusion.68
  110.5 2.5 copy.34
  113.0 1.5 subtract_convert_fusion.1
  114.6 0.3 copy-done.4
  114.9 1.7 fusion.45
  116.6 5.7 %fusion.69 = (f32[8,512]{1,0:T(8,128)S(1)}, f32[8,512,512]{1,2,0:T(8,128)}) fusion(f32[8,512,512]{1,2,0:T(8,128)S(1)} %fusion.45, pred[512,512]{0,1:T(8,128)(4,1)S(1)} %copy-done.13), kind=kOutput, calls=%fused_computation.108 | output fusion | flops 12583423 | bytes 17055744 | tf_op jit(solution)/shard_map/sub | solution.py:130
  122.4 5.4 %fusion.46 = f32[8,512,512]{2,1,0:T(8,128)} fusion(bf16[512,8,128]{0,2,1:T(8,128)(2,1)S(1)} %bitcast.62, bf16[512,8,128]{2,1,0:T(8,128)(2,1)S(1)} %copy-done.2), kind=kOutput, calls=%fused_computation.55 | convolution fusion | flops 536870912 | bytes 10485760 | tf_op jit(solution)/shard_map/qhd,khd->hqk/dot_general | solution.py:134
  127.8 0.8 copy-done.22
  128.5 2.5 fusion.42
  131.0 15.9 %fusion.32 = f32[512,8,192]{0,2,1:T(8,128)} fusion(f32[8,512,512]{2,1,0:T(8,128)} %fusion.46, bf16[512,8,32]{0,2,1:T(8,128)(2,1)} %copy-done.9, bf16[512,8,32]{0,2,1:T(8,128)(2,1)S(1)} %get-tuple-element.13, bf16[512,8,128]{0,2,1:T(8,128)(2,1)} %slice.105, f32[8,512,512]{1,2,0:T(8,128)} %get-tuple-element.23, f32[8,512]{1,0:T(8,128)} %copy-done.23), kind=kOutput, calls=%fused_computation.42 | convolution fusion | flops 824709632 | bytes 21512192 | tf_op jit(solution)/shard_map/hqk,qhd->khd/dot_general | solution.py:138
  146.9 1.7 slice.164
  148.7 1.4 pad_maximum_fusion.1
  150.0 3.3 fusion.67
  153.3 2.9 multiply_reduce_fusion
  156.2 0.1 copy.30
  156.3 4.7 %pad_maximum_fusion = f32[512,2049]{1,0:T(8,128)} fusion(f32[512,1]{1,0:T(8,128)S(1)} %copy.30, f32[512,2048]{1,0:T(8,128)} %fusion.67), kind=kLoop, calls=%fused_computation.15 | loop fusion | flops 1049088 | bytes 8392704 | tf_op jit(solution)/shard_map/concatenate | solution.py:55
  161.1 0.6 copy-done.24
  161.8 14.6 %fusion.31 = f32[512,8,192]{0,2,1:T(8,128)} fusion(f32[8,512,512]{2,1,0:T(8,128)} %fusion.46, bf16[512,8,64]{0,2,1:T(8,128)(2,1)} %copy-done.5, bf16[512,8,128]{0,2,1:T(8,128)(2,1)} %copy.34, f32[8,512,512]{1,2,0:T(8,128)} %get-tuple-element.23, f32[8,512]{1,0:T(8,128)S(1)} %copy-done.24), kind=kOutput, calls=%fused_computation.41 | convolution fusion | flops 823136768 | bytes 21512192 | tf_op jit(solution)/shard_map/hqk,khd->qhd/dot_general | solution.py:137
  176.4 1.8 slice.165
  178.2 1.4 slice_reduce_fusion
  179.6 1.4 subtract_convert_fusion
  181.0 0.1 pad_maximum_fusion.4
  181.2 0.3 subtract_convert_fusion.2
  181.5 0.2 multiply_convert_fusion
  181.8 0.5 copy-done.6
  182.3 0.3 copy-done.11
  182.6 11.7 %convolution_bitcast_fusion = f32[2048,2112]{0,1:T(8,128)} fusion(bf16[512,2048]{1,0:T(8,128)(2,1)S(1)} %copy-done, bf16[512,32]{0,1:T(8,128)(2,1)S(1)} %get-tuple-element.16, bf16[512,32]{0,1:T(8,128)(2,1)S(1)} %get-tuple-element.15, bf16[512,512]{0,1:T(8,128)(2,1)S(1)} %multiply_convert_fusion, bf16[512,1536]{0,1:T(8,128)(2,1)S(1)} %bitcast.65), kind=kOutput, calls=%fused_computation.2 | convolution fusion | flops 4437835776 | bytes 21561344 | tf_op jit(solution)/shard_map/dot_general | solution.py:177
  194.3 43.9 %reduce-scatter.5.cloned.1.call-done = f32[32,2049]{1,0:T(8,128)} async-done(((f32[512,2049]{1,0:T(8,128)}), f32[32,2049]{1,0:T(8,128)}) %reduce-scatter.5.cloned.1.call-update) | async-done | bytes 262288 | tf_op jit(solution)/shard_map/reduce_scatter | solution.py:56
  238.3 1.8 reshape.152
  240.0 6.8 %all-to-all-start.1 = ((f32[8,4,2049]{2,1,0:T(4,128)}), f32[8,4,2049]{2,1,0:T(4,128)S(1)}, u32[]{:S(2)}, u32[]{:S(2)}) async-start(f32[8,4,2049]{2,1,0:T(4,128)} %reshape.152), calls=%async_computation.3 | async-start | bytes 557056 | tf_op jit(solution)/shard_map/all_to_all | solution.py:49
  246.8 108.7 %reduce-scatter.3.cloned.1.call-done = f32[128,2112]{0,1:T(8,128)} async-done(((f32[2048,2112]{0,1:T(8,128)}), f32[128,2112]{0,1:T(8,128)}) %reduce-scatter.3.cloned.1.call-update) | async-done | bytes 1081360 | tf_op jit(solution)/shard_map/reduce_scatter | solution.py:176
  355.5 2.6 copy.29
  358.1 5.4 %all-to-all-start = ((f32[8,16,2112]{2,1,0:T(8,128)}), f32[8,16,2112]{2,1,0:T(8,128)S(1)}, u32[]{:S(2)}, u32[]{:S(2)}) async-start(f32[8,16,2112]{2,1,0:T(8,128)} %bitcast.12), calls=%async_computation.1 | async-start | bytes 2228224 | tf_op jit(solution)/shard_map/all_to_all | solution.py:49
  363.6 0.7 multiply_reduce_fusion.6
  364.2 0.6 multiply_reduce_fusion.4
  364.9 14.3 %all-to-all-done = f32[8,16,2112]{2,1,0:T(8,128)S(1)} async-done(((f32[8,16,2112]{2,1,0:T(8,128)}), f32[8,16,2112]{2,1,0:T(8,128)S(1)}, u32[]{:S(2)}, u32[]{:S(2)}) %all-to-all-start) | async-done | bytes 1081376 | tf_op jit(solution)/shard_map/all_to_all | solution.py:49
  379.2 0.6 multiply_reduce_fusion.3
  381.9 8.7 %psum.28 = f32[]{:T(128)} all-reduce(f32[]{:T(128)S(6)} %add.54), channel_id=1, replica_groups=mesh['node_0'=4,'node_1'=4,'local_0'=4,'local_1'=2] {'node_0'}, use_global_device_ids=true, to_apply=%region_14.15 | all-reduce | flops 1 | bytes 8 | tf_op jit(solution)/shard_map/psum | solution.py:77
  390.5 7.3 %psum.29 = f32[]{:T(128)} all-reduce(f32[]{:T(128)} %psum.28), channel_id=1, replica_groups=mesh['node_0'=4,'node_1'=4,'local_0'=4,'local_1'=2] {'node_1'}, use_global_device_ids=true, to_apply=%region_15.16 | all-reduce | flops 1 | bytes 8 | tf_op jit(solution)/shard_map/psum | solution.py:77
  397.9 8.7 %fusion.6 = f32[512,2048]{1,0:T(8,128)} fusion(bf16[512,1536]{0,1:T(8,128)(2,1)} %bitcast.66, bf16[2048,2112]{1,0:T(8,128)(2,1)} %all-gather.3.cloned.1.call-done), kind=kOutput, calls=%fused_computation.11 | convolution fusion | flops 3221225472 | bytes 12058624 | tf_op jit(solution)/shard_map/dot_general | solution.py:96
  406.6 7.5 %psum.30 = f32[]{:T(128)} all-reduce(f32[]{:T(128)} %psum.29), channel_id=1, replica_groups=mesh['node_0'=4,'node_1'=4,'local_0'=4,'local_1'=2] {'local_0'}, use_global_device_ids=true, to_apply=%region_16.17 | all-reduce | flops 1 | bytes 8 | tf_op jit(solution)/shard_map/psum | solution.py:77
  414.1 6.2 %add_convert_fusion = bf16[512,2048]{1,0:T(8,128)(2,1)} fusion(f32[512,2048]{1,0:T(8,128)} %fusion.6, bf16[2048,2112]{1,0:T(8,128)(2,1)} %all-gather.3.cloned.1.call-done, bf16[512,32]{0,1:T(8,128)(2,1)S(1)} %copy-done.18, bf16[512,32]{0,1:T(8,128)(2,1)S(1)} %copy-done.16, bf16[512,512]{0,1:T(8,128)(2,1)S(1)} %copy-done.12), kind=kOutput, calls=%fused_computation.16 | convolution fusion | flops 1211826176 | bytes 9502720 | tf_op jit(solution)/shard_map/dot_general | solution.py:96
  420.2 9.6 %psum.31 = f32[]{:T(128)} all-reduce(f32[]{:T(128)} %psum.30), channel_id=1, replica_groups=mesh['node_0'=4,'node_1'=4,'local_0'=4,'local_1'=2] {'local_1'}, use_global_device_ids=true, to_apply=%region_17.18 | all-reduce | flops 1 | bytes 8 | tf_op jit(solution)/shard_map/psum | solution.py:77
  430.6 0.6 multiply_reduce_fusion.5
  431.2 0.6 slice_multiply_fusion.3
  431.8 0.6 slice_multiply_fusion.2
  432.4 0.6 slice_multiply_fusion.1
  (61 shorter events, 0.5 us)
Async XLA Ops:
  7.2 86.5 %copy-start = (bf16[512,2048]{1,0:T(8,128)(2,1)S(1)}, bf16[512,2048]{1,0:T(8,128)(2,1)}, u32[]{:S(2)}) copy-start(bf16[512,2048]{1,0:T(8,128)(2,1)} %param.6) | copy-start | bytes 6291460
  7.2 6.2 %copy-start.7 = (bf16[512,1024]{1,0:T(8,128)(2,1)S(1)}, bf16[512,1024]{1,0:T(8,128)(2,1)}, u32[]{:S(2)}) copy-start(bf16[512,1024]{1,0:T(8,128)(2,1)} %param.7) | copy-start | bytes 3145732
  7.2 31.9 %all-gather.5.cloned.1.call-start = ((), (), s32[]{:S(2)}) async-start(), calls=%async_computation.5 | async-start | bytes 2506752 | tf_op jit(solution)/shard_map/all_gather | solution.py:27
  9.9 83.8 %all-gather.3.cloned.1.call-start = ((), (), s32[]{:S(2)}) async-start(), calls=%async_computation.4 | async-start | bytes 10027008 | tf_op jit(solution)/shard_map/all_gather | solution.py:38
  13.3 224.9 %reduce-scatter.5.cloned.1.call-start = ((), (), s32[]{:S(2)}) async-start(), calls=%async_computation.7 | async-start | bytes 4734976 | tf_op jit(solution)/shard_map/reduce_scatter | solution.py:56
  102.3 4.7 %copy-start.19 = (bf16[512,2049]{1,0:T(8,128)(2,1)S(1)}, bf16[512,2049]{1,0:T(8,128)(2,1)}, u32[]{:S(2)}) copy-start(bf16[512,2049]{1,0:T(8,128)(2,1)} %all-gather.5.cloned.1.call-done) | copy-start | bytes 6294532
  113.0 1.6 copy-start.3
  113.0 1.9 copy-start.4
  114.5 2.0 copy-start.9
  114.9 1.7 copy-start.5
  114.9 1.7 copy-start.13
  116.6 5.7 %copy-start.1 = (bf16[512,1024]{0,1:T(8,128)(2,1)S(1)}, bf16[512,1024]{0,1:T(8,128)(2,1)}, u32[]{:S(2)}) copy-start(bf16[512,1024]{0,1:T(8,128)(2,1)} %copy.36) | copy-start | bytes 3145732
  116.6 5.7 %copy-start.2 = (bf16[512,8,128]{2,1,0:T(8,128)(2,1)S(1)}, bf16[512,8,128]{2,1,0:T(8,128)(2,1)}, u32[]{:S(2)}) copy-start(bf16[512,8,128]{2,1,0:T(8,128)(2,1)} %get-tuple-element.10) | copy-start | bytes 3145732
  122.3 5.4 %copy-start.23 = (f32[8,512]{1,0:T(8,128)}, f32[8,512]{1,0:T(8,128)S(1)}, u32[]{:S(2)}) copy-start(f32[8,512]{1,0:T(8,128)S(1)} %get-tuple-element.22) | copy-start | bytes 49156
  122.4 6.2 %copy-start.22 = (f32[8,512,512]{1,2,0:T(8,128)S(1)}, f32[8,512,512]{1,2,0:T(8,128)}, u32[]{:S(2)}) copy-start(f32[8,512,512]{1,2,0:T(8,128)} %get-tuple-element.23) | copy-start | bytes 25165828
  150.0 3.3 copy-start.20
  161.0 0.7 copy-start.24
  161.1 194.5 %reduce-scatter.3.cloned.1.call-start = ((), (), s32[]{:S(2)}) async-start(), calls=%async_computation.6 | async-start | bytes 18382848 | tf_op jit(solution)/shard_map/reduce_scatter | solution.py:176
  176.4 3.2 copy-start.10
  176.4 3.2 copy-start.14
  178.2 3.0 copy-start.21
  178.2 3.3 copy-start.8
  181.1 1.1 copy-start.6
  181.5 12.8 %copy-start.15 = (bf16[512,32]{0,1:T(8,128)(2,1)}, bf16[512,32]{0,1:T(8,128)(2,1)S(1)}, u32[]{:S(2)}) copy-start(bf16[512,32]{0,1:T(8,128)(2,1)S(1)} %get-tuple-element.15) | copy-start | bytes 98308
  181.5 12.8 %copy-start.17 = (bf16[512,32]{0,1:T(8,128)(2,1)}, bf16[512,32]{0,1:T(8,128)(2,1)S(1)}, u32[]{:S(2)}) copy-start(bf16[512,32]{0,1:T(8,128)(2,1)S(1)} %get-tuple-element.16) | copy-start | bytes 98308
  181.8 0.8 copy-start.11
  240.0 118.1 %all-to-all-start.1 = ((f32[8,4,2049]{2,1,0:T(4,128)}), f32[8,4,2049]{2,1,0:T(4,128)S(1)}, u32[]{:S(2)}, u32[]{:S(2)}) async-start(f32[8,4,2049]{2,1,0:T(4,128)} %reshape.152), calls=%async_computation.3 | async-start | bytes 557056 | tf_op jit(solution)/shard_map/all_to_all | solution.py:49
  358.1 21.0 %all-to-all-start = ((f32[8,16,2112]{2,1,0:T(8,128)}), f32[8,16,2112]{2,1,0:T(8,128)S(1)}, u32[]{:S(2)}, u32[]{:S(2)}) async-start(f32[8,16,2112]{2,1,0:T(8,128)} %bitcast.12), calls=%async_computation.1 | async-start | bytes 2228224 | tf_op jit(solution)/shard_map/all_to_all | solution.py:49
  397.8 16.2 %copy-start.12 = (bf16[512,512]{0,1:T(8,128)(2,1)S(1)}, bf16[512,512]{0,1:T(8,128)(2,1)}, u32[]{:S(2)}) copy-start(bf16[512,512]{0,1:T(8,128)(2,1)} %copy-done.11) | copy-start | bytes 1572868
  397.8 16.2 %copy-start.16 = (bf16[512,32]{0,1:T(8,128)(2,1)S(1)}, bf16[512,32]{0,1:T(8,128)(2,1)}, u32[]{:S(2)}) copy-start(bf16[512,32]{0,1:T(8,128)(2,1)} %copy-done.15) | copy-start | bytes 98308
  397.8 16.2 %copy-start.18 = (bf16[512,32]{0,1:T(8,128)(2,1)S(1)}, bf16[512,32]{0,1:T(8,128)(2,1)}, u32[]{:S(2)}) copy-start(bf16[512,32]{0,1:T(8,128)(2,1)} %copy-done.17) | copy-start | bytes 98308
Sparse Core Ops, SparseCore 0:
  10.0 29.0 all-gather.4
  41.3 52.2 all-gather.2
  161.2 77.0 reduce-scatter.4
  241.6 113.9 reduce-scatter.2
where the time goes:
time: 441 us; the launch traced here: 440 us
  waiting for transfers between devices  244 us (55%)
  matrix products  84.2 us (19%)
  blocking collectives  33.1 us (8%)
  other arithmetic  29.2 us (7%)
  local copies, waits for them, and re-layouts  19.8 us (4%)
  between operations  16.8 us (4%)
  starting transfers between devices  12.3 us (3%)
    reduce_scatter x1, waiting for transfers between devices, per_device(): lax.psum_scatter(lax.dot_general(tokens, joined, (((0,), (0,)), ((), ()))...  109 us
    all_gather x1, waiting for transfers between devices, sent_together_2(): filled = lax.all_gather(both, axis, axis=dim, tiled=True)  53.6 us
    reduce_scatter x1, waiting for transfers between devices, sent_together_3(): lax.psum_scatter(both, axis, scatter_dimension=dim, tiled=True)  43.9 us
    psum x4, blocking collectives, one_axis_at_a_time(): shard = lax.psum(shard, axis)  33.1 us
    all_gather x1, waiting for transfers between devices, sent_together(): lax.all_gather(both, axis, axis=dim, tiled=True)  23.5 us
    dot_general x3, matrix products, transposed_product(): lax.dot_general(left, right, (((1,), (1,)), ((), ())), preferred_element_...  17.8 us
    dot_general x1, matrix products, local_backward(): jnp.einsum('hqk,qhd->khd', dscores, query_full, preferred_element_type=jn...  15.9 us
    dot_general x1, matrix products, local_backward(): jnp.einsum('hqk,khd->qhd', dscores, key_full, preferred_element_type=jnp....  14.6 us
  transfers between devices with their start and end apart: 6, of which 5 were waited for; matrix products, arithmetic and copies ran while one was open for 10% of the time, Pallas kernels for 0%

commit v1 on v0

v1 whole, which is shorter than its diff:
```python
import math

import jax
import jax.numpy as jnp
import numpy as np
from jax import lax
from jax.experimental import pallas as pl
from jax.experimental.pallas import tpu as pltpu
from jax.sharding import Mesh
from jax.sharding import PartitionSpec as P

H = 8
DN = 128
DR = 64
DV = 128
KVL = 512
SEQ = 512
D = 2048
NPARAM = 5374464
EPSILON = 1e-06
ROPE_BASE = 10000.0
LOCAL = ("local_0", "local_1")
NODE_LOCAL = ("node_0", "node_1", "local_0", "local_1")
MESH = pl.DeviceIdType.MESH
AZ, AX, AY, AC = NODE_LOCAL

WCOL = 2176
SCALE = 1.0 / math.sqrt(DN + DR)
GROUPS = ((512, AZ, AX, AY), (512, AX, AY, AZ), (384, AY, AZ, AX))
GOFF = (0, 512, 1024)
GTOT = 1408
F32 = jnp.float32
BF16 = jnp.bfloat16


def rope_constants():
    position = np.arange(SEQ, dtype=np.float32)[:, None]
    freq = np.float32(ROPE_BASE) ** (-np.arange(DR // 2, dtype=np.float32) * np.float32(2.0 / DR))
    angle = (position * freq[None, :].astype(np.float32)).astype(np.float32)
    cosine = np.cos(angle).astype(np.float32)
    sine = np.sin(angle).astype(np.float32)
    return np.concatenate([cosine] * 4, 1), np.concatenate([-sine, sine] * 2, 1)


def nt(a, b):
    return lax.dot_general(a, b, (((1,), (1,)), ((), ())), preferred_element_type=F32)


def nn(a, b):
    return jnp.dot(a, b, preferred_element_type=F32)


def tn(a, b):
    return lax.dot_general(a, b, (((0,), (0,)), ((), ())), preferred_element_type=F32)


def mega(
    tokens_hbm, dout_hbm, cos_hbm, sin_hbm, wq_ref, wd_ref, wu_ref, gain_ref,
    fin_ref, clip_ref, tg_hbm,
    tokens, dout, cosr, sinr, wbuf, ubuf, gbuf, tokt, acc, qrope, qnope, nrm, nrt, ng, krp, dkr,
    jb, jp, kvg, kvgp, rg, rgp, rgf, invr, gmat, tgb,
    p0, p1, p2, own0, own1, own2, rx0, rx1, rx2, ra0, ra1, ra2,
    q0, q1, q2, rx20, rx21, rx22, ra20, ra21, ra22,
    s0, s1, s2, rx30, rx31, rx32, ra30, ra31, ra32,
    nbuf, lsem, ssem, rsem,
):
    iz, ix, iy, ic = (lax.axis_index(a) for a in NODE_LOCAL)
    at = {AZ: iz, AX: ix, AY: iy}
    other = 1 - ic

    def step(axis, by):
        return lax.rem(at[axis] + (by + 4), 4)

    sends = []
    table = {}

    def sem_of(key):
        return table.setdefault(key, len(table))

    def send(key, src, dst, peer):
        k = sem_of(key)
        d = pltpu.make_async_remote_copy(
            src_ref=src, dst_ref=dst, send_sem=ssem.at[k], recv_sem=rsem.at[k],
            device_id=peer, device_id_type=MESH)
        d.start()
        sends.append(d)

    def arrived(key, dst):
        k = sem_of(key)
        pltpu.make_async_remote_copy(
            src_ref=dst, dst_ref=dst, send_sem=ssem.at[k], recv_sem=rsem.at[k],
            device_id={AC: other}, device_id_type=MESH).wait_recv()

    mate = {AC: other}
    locals_ = []
    for n, (src, dst) in enumerate(((tokens_hbm, tokens), (dout_hbm, dout), (cos_hbm, cosr), (sin_hbm, sinr))):
        d = pltpu.make_async_copy(src, dst, lsem.at[n])
        d.start()
        locals_.append(d)

    barrier = pltpu.get_barrier_semaphore()
    for axis in (AZ, AX, AY):
        for by in (1, -1, 2):
            pl.semaphore_signal(barrier, inc=1, device_id={axis: step(axis, by)}, device_id_type=MESH)
    pl.semaphore_signal(barrier, inc=1, device_id=mate, device_id_type=MESH)

    for h in range(H):
        wbuf[iy, ic, :, :, h * 128:(h + 1) * 128] = wq_ref[:, h * 192:h * 192 + 128].reshape(8, 32, 128)
    for h in range(0, H, 2):
        pair = jnp.concatenate(
            [wq_ref[:, h * 192 + 128:h * 192 + 192], wq_ref[:, h * 192 + 320:h * 192 + 384]], 1)
        wbuf[iy, ic, :, :, 1024 + h * 64:1024 + h * 64 + 128] = pair.reshape(8, 32, 128)
    wbuf[iy, ic, :, :, 1536:2048] = wd_ref[:, :512].reshape(8, 32, 512)
    last = jnp.concatenate([wd_ref[:, 512:576], jnp.zeros((256, 64), BF16)], 1)
    wbuf[iy, ic, :, :, 2048:2176] = last.reshape(8, 32, 128)
    for p in range(8):
        ubuf[iy, ic, p] = wu_ref[:, p * 256:(p + 1) * 256]
    gbuf[iy, ic] = jnp.broadcast_to(
        jnp.concatenate([gain_ref[...].astype(F32), jnp.zeros((1, 64), F32)], 1), (8, 128))
    pl.semaphore_wait(barrier, 10)

    RING = (AX, AZ)
    YO = (step(AY, -1), step(AY, 1), step(AY, 2))

    def wpiece(yy, k, q):
        return wbuf.at[yy, ic, k * 4 + q]

    def upiece(yy, k, q):
        return ubuf.at[yy, ic, k * 4 + q]

    def halves(ref, rows):
        return ref.at[0:rows // 2], ref.at[rows // 2:rows]

    KIND = {"w": (wpiece, 32), "u": (upiece, 64)}

    def y_send(kind, k):
        piece, _ = KIND[kind]
        r = piece(iy, k, at[RING[k]])
        send((kind, "y", k, 0), r, r, {AY: step(AY, 1)})
        send((kind, "y", k, 1), r, r, {AY: step(AY, -1)})

    def p_send(kind, k, yo):
        piece, _ = KIND[kind]
        r = piece(YO[yo], k, at[RING[k]])
        send((kind, "p", k, yo, 0), r, r, {RING[k]: step(RING[k], 1)})
        send((kind, "p", k, yo, 1), r, r, {RING[k]: step(RING[k], -1)})

    def y_take(kind, k, d):
        piece, rows = KIND[kind]
        r = piece(YO[d], k, at[RING[k]])
        arrived((kind, "y", k, d), r)
        half = halves(r, rows)[d]
        send((kind, "y2", k, d), half, half, {AY: step(AY, 1 if d == 0 else -1)})
        p_send(kind, k, d)

    def y2_take(kind, k):
        piece, rows = KIND[kind]
        r = piece(YO[2], k, at[RING[k]])
        for d in range(2):
            arrived((kind, "y2", k, d), halves(r, rows)[d])
        p_send(kind, k, 2)

    def p_take(kind, k, yo):
        piece, rows = KIND[kind]
        for d in range(2):
            r = piece(YO[yo], k, step(RING[k], -1 if d == 0 else 1))
            arrived((kind, "p", k, yo, d), r)
            half = halves(r, rows)[d]
            send((kind, "p2", k, yo, d), half, half, {RING[k]: step(RING[k], 1 if d == 0 else -1)})

    def p2_take(kind, k, yo):
        piece, rows = KIND[kind]
        r = piece(YO[yo], k, step(RING[k], 2))
        for d in range(2):
            arrived((kind, "p2", k, yo, d), halves(r, rows)[d])

    def to_mate(kind, yo):
        buf = wbuf if kind == "w" else ubuf
        yy = iy if yo is None else YO[yo]
        send((kind, "d", yo), buf.at[yy, ic], buf.at[yy, ic], mate)

    def from_mate(kind, yo):
        buf = wbuf if kind == "w" else ubuf
        yy = iy if yo is None else YO[yo]
        arrived((kind, "d", yo), buf.at[yy, other])

    def project(yo):
        yy = iy if yo is None else YO[yo]
        left = tokens[:, pl.ds(pl.multiple_of(yy * 512, 512), 512)]
        for lo, hi in ((0, 768), (768, 1536), (1536, 2176)):
            w = wbuf[yy, :, :, :, lo:hi].reshape(512, hi - lo)
            if yo is None:
                acc[:, lo:hi] = nn(left, w)
            else:
                acc[:, lo:hi] += nn(left, w)

    for k in range(2):
        y_send("w", k)
    to_mate("w", None)
    to_mate("u", None)
    g = gbuf.at[iy, ic]
    for n, by in enumerate((1, -1, 2)):
        send(("g", n), g, g, {AY: step(AY, by)})
    send(("gd", 3), g, g, mate)

    locals_[0].wait()

    for z in range(4):
        tokt[0, z] = tokens[:, z * 512:(z + 1) * 512].T.reshape(4, 4, 32, 512)
    for k in range(2):
        for d in range(2):
            y_take("w", k, d)
    for k in range(2):
        y_send("u", k)
    send(("tok",), tokt.at[0], tokt.at[1], mate)
    from_mate("w", None)
    project(None)
    for k in range(2):
        y2_take("w", k)
    for k in range(2):
        p_take("w", k, 0)
    for k in range(2):
        for d in range(2):
            y_take("u", k, d)
    for k in range(2):
        p_take("w", k, 1)
    for k in range(2):
        p2_take("w", k, 0)
    to_mate("w", 0)
    for k in range(2):
        y2_take("u", k)
    for k in range(2):
        p2_take("w", k, 1)
    to_mate("w", 1)
    for k in range(2):
        p_take("w", k, 2)
    for yo in range(2):
        for k in range(2):
            p_take("u", k, yo)
    from_mate("w", 0)
    project(0)
    for k in range(2):
        p2_take("w", k, 2)
    to_mate("w", 2)
    for k in range(2):
        p_take("u", k, 2)
    from_mate("w", 1)
    project(1)
    for n, by in enumerate((-1, 1, 2)):
        gg = gbuf.at[step(AY, by), ic]
        arrived(("g", n), gg)
        send(("gd", n), gg, gg, mate)
    for yo in range(3):
        for k in range(2):
            p2_take("u", k, yo)
        to_mate("u", yo)
    from_mate("w", 2)
    project(2)
    for n, by in enumerate((-1, 1, 2)):
        arrived(("gd", n), gbuf.at[step(AY, by), other])
    arrived(("gd", 3), gbuf.at[iy, other])

    for d in locals_[1:]:
        d.wait()

    lane = lax.broadcasted_iota(jnp.int32, (1, 128), 1)
    low = lax.rem(lane, 64) < 32

    def swap(v):
        return jnp.where(low, pltpu.roll(v, 96, 1), pltpu.roll(v, 32, 1))

    def rot(v, sign):
        return v * cosr[...] + swap(v) * (sinr[...] * sign)

    gain = jnp.concatenate([gbuf[y, c, 0:1, 0:64] for y in range(4) for c in range(2)], 1)
    for n in range(4):
        cols = slice(1024 + n * 128, 1152 + n * 128)
        qrope[:, n * 128:(n + 1) * 128] = rot(acc[:, cols].astype(BF16).astype(F32), 1.0).astype(BF16)
    for n in range(8):
        qnope[:, n * 128:(n + 1) * 128] = acc[:, n * 128:(n + 1) * 128].astype(BF16)
    kr = rot(acc[:, 2048:2176], 1.0)
    krp[0] = jnp.where(lane < 64, kr, 0.0).astype(BF16)
    krp[1] = jnp.where(lane < 64, 0.0, pltpu.roll(kr, 64, 1)).astype(BF16)
    for n in range(4):
        rows = slice(n * 128, (n + 1) * 128)
        latent = acc[rows, 1536:2048]
        inv = lax.rsqrt(jnp.mean(latent * latent, axis=-1, keepdims=True) + EPSILON)
        unit = latent * inv
        acc[rows, 1536:2048] = unit
        invr[rows] = jnp.broadcast_to(inv, (128, 128))
        nrm[rows] = (unit * gain).astype(BF16)
    nrt[0] = nrm[...].T
    send(("nrt",), nrt.at[0], nrt.at[1], mate)
    ng[...] = jnp.zeros((512, 512), F32)
    dkr[...] = jnp.zeros((512, 128), F32)
    for yo in range(3):
        from_mate("u", yo)
    from_mate("u", None)

    tri = (lax.broadcasted_iota(jnp.int32, (256, 256), 0)
           <= lax.broadcasted_iota(jnp.int32, (256, 256), 1))

    def block(kf, v, qf, do, diag):
        rows = kf.shape[0]
        s = nt(kf, qf) * SCALE
        masked = jnp.where(tri, s[rows - 256:], -1e30)
        s = masked if rows == 256 else jnp.concatenate([s[:rows - 256], masked], 0)
        w = jnp.exp(s - jnp.max(s, axis=0, keepdims=True))
        probs = w * (1.0 / jnp.sum(w, axis=0, keepdims=True))
        dp = nt(v, do)
        delta = jnp.sum(probs * dp, axis=0, keepdims=True)
        ds = (probs * (dp - delta) * SCALE).astype(BF16)
        return probs.astype(BF16), ds

    def pair(n, carry):
        rope_cols = pl.ds(pl.multiple_of(n * 128, 128), 128)
        qr = qrope[:, rope_cols]
        total = None
        for e in range(2):
            h = 2 * n + e
            hc = pl.ds(pl.multiple_of(h * 128, 128), 128)
            u = ubuf[:, :, h].reshape(512, 256)
            kv = nn(nrm[...], u).astype(BF16)
            kf = jnp.concatenate([kv[:, :128], krp[e]], 1)
            v = kv[:, 128:]
            qf = jnp.concatenate([qnope[:, hc], qr], 1)
            do = dout[:, hc]
            pa, da = block(kf[:256], v[:256], qf[:256], do[:256], True)
            pb, db = block(kf, v, qf[256:], do[256:], False)
            dv = nn(pb, do[256:])
            dv = jnp.concatenate([dv[:256] + nn(pa, do[:256]), dv[256:]], 0)
            dk = nn(db, qf[256:])
            dk = jnp.concatenate([dk[:256] + nn(da, qf[:256]), dk[256:]], 0)
            dq = jnp.concatenate([tn(da, kf[:256]), tn(db, kf)], 0)
            jb[0, :, hc] = dq[:, :128].astype(BF16)
            total = dq[:, 128:] if e == 0 else total + dq[:, 128:]
            keep = lane < 64 if e == 0 else lane >= 64
            dkr[...] += jnp.where(keep, dk[:, 128:], 0.0)
            half, j = n // 2, lax.rem(n, 2) * 2 + e
            jc = pl.ds(pl.multiple_of(j * 128, 128), 128)
            kg = dk[:, :128].astype(BF16)
            vg = dv.astype(BF16)
            kvg[half, 0, :, jc] = kg
            kvg[half, 1, :, jc] = vg
            ng[...] += nt(jnp.concatenate([kg, vg], 1), u)
        jb[1, :, rope_cols] = rot(total, -1.0).astype(BF16)
        return carry

    lax.fori_loop(0, 4, pair, 0)
    send(("kvg",), kvg.at[other], kvgp, mate)

    gterm = jnp.zeros((1, 512), F32)
    for n in range(4):
        rows = slice(n * 128, (n + 1) * 128)
        unit = acc[rows, 1536:2048]
        grad = ng[rows]
        gterm = gterm + jnp.sum(grad * unit, axis=0, keepdims=True)
        scaled = grad * gain
        inner = jnp.mean(scaled * unit, axis=-1, keepdims=True)
        jb[1, rows, 512:1024] = (invr[rows, 0:1] * (scaled - unit * inner)).astype(BF16)
    dk = dkr[...]
    rope = jnp.where(lane < 64, rot(dk + pltpu.roll(dk, 64, 1), -1.0), 0.0)
    rgf[...] = rope.astype(BF16)
    rg[0] = jnp.where(lane < 32, rope, 0.0).astype(BF16)
    rg[1] = jnp.where(lane < 32, pltpu.roll(rope, 96, 1), 0.0).astype(BF16)
    send(("j",), jb.at[other], jp, mate)
    send(("rg",), rg.at[other], rgp, mate)
    column = jnp.broadcast_to(gterm, (128, 512)).T
    column = jnp.where(lane == 32, column, 0.0).reshape(64, 8, 128)
    gmat[...] = jnp.concatenate([column, jnp.zeros((64, 24, 128), F32)], 1).reshape(4, 4, 4, 32, 128)

    tgd = []

    def token_block(n):
        yy, cc = n // 2, n % 2
        w = wbuf[yy, cc].reshape(256, WCOL)
        out = nt(jb[0], w[:, :1024]) + nt(jb[1], w[:, 1024:2048]) + nt(rgf[...], w[:, 2048:])
        tgb[n] = out.astype(BF16)
        d = pltpu.make_async_copy(tgb.at[n], tg_hbm.at[:, n * 256:(n + 1) * 256], lsem.at[4 + n])
        d.start()
        tgd.append(d)

    for n in range(3):
        token_block(n)
    arrived(("tok",), tokt.at[1])
    arrived(("nrt",), nrt.at[1])
    arrived(("kvg",), kvgp)
    arrived(("j",), jp)
    arrived(("rg",), rgp)

    pb = (p0, p1, p2)
    own = (own0, own1, own2)

    def chunk(g, t):
        lo = g * 384
        width = 384 if g < 2 else 256
        total = None
        for n in range(2):
            src = (tokt.at[n, t], tokt.at[n, :, t], tokt.at[n, :, :, t])[g]
            left = src[...].reshape(512, 512)
            right = jb[ic, :, lo:lo + width] if n == 0 else jp[:, lo:lo + width]
            if g == 2:
                right = jnp.concatenate([right, rg[ic] if n == 0 else rgp[...]], 1)
            term = nn(left, right)
            total = term if n == 0 else total + term
        total = total.reshape(4, 4, 32, 384)
        if g == 2:
            total = jnp.concatenate([total[..., :256], total[..., 256:] + gmat[:, :, t]], -1)
            return total
        up = None
        for n in range(2):
            src = (nrt.at[n, pl.ds(pl.multiple_of(t * 128, 128), 128)] if g == 0 else None)
            if g == 0:
                left = src[...]
            else:
                left = jnp.concatenate(
                    [nrt[n, pl.ds(pl.multiple_of(z * 128 + t * 32, 32), 32)] for z in range(4)], 0)
            term = nn(left, kvg[ic, g] if n == 0 else kvgp[g])
            up = term if n == 0 else up + term
        up = up.reshape(16, 8, 512)
        up = jnp.concatenate([up[:, :, j * 128:(j + 1) * 128] for j in range(4)], 1)
        return jnp.concatenate([total, up.reshape(4, 4, 32, 128)], -1)

    rx = (rx0, rx1, rx2)
    ra = (ra0, ra1, ra2)
    for by in (2, 1, -1, 0):
        for g, (width, a1, a2, a3) in enumerate(GROUPS):
            t = step(a1, by)
            value = chunk(g, t)
            right, left = {a1: step(a1, 1)}, {a1: step(a1, -1)}
            if by == 0:
                own[g][...] = value
                continue
            slot = {2: 0, 1: 1, -1: 2}[by]
            pb[g][slot] = value.astype(BF16)
            if by == 2:
                send((1, g, "x", 0), pb[g].at[0, 0:2], rx[g].at[0], right)
                send((1, g, "x", 1), pb[g].at[0, 2:4], rx[g].at[1], left)
            elif by == 1:
                send((1, g, "a", 0, 1), pb[g].at[1, 2:4], ra[g].at[0, 2:4], right)
            else:
                send((1, g, "a", 1, 0), pb[g].at[2, 0:2], ra[g].at[1, 0:2], left)
    for g, (width, a1, a2, a3) in enumerate(GROUPS):
        right, left = {a1: step(a1, 1)}, {a1: step(a1, -1)}
        arrived((1, g, "x", 0), rx[g].at[0])
        pb[g][1, 0:2] = (pb[g][1, 0:2].astype(F32) + rx[g][0].astype(F32)).astype(BF16)
        arrived((1, g, "x", 1), rx[g].at[1])
        pb[g][2, 2:4] = (pb[g][2, 2:4].astype(F32) + rx[g][1].astype(F32)).astype(BF16)
        send((1, g, "a", 0, 0), pb[g].at[1, 0:2], ra[g].at[0, 0:2], right)
        send((1, g, "a", 1, 1), pb[g].at[2, 2:4], ra[g].at[1, 2:4], left)
    for n in range(3, 8):
        token_block(n)

    q = (q0, q1, q2)
    rx2_ = (rx20, rx21, rx22)
    ra2_ = (ra20, ra21, ra22)
    for g, (width, a1, a2, a3) in enumerate(GROUPS):
        for d in range(2):
            for h in range(2):
                arrived((1, g, "a", d, h), ra[g].at[d, h * 2:h * 2 + 2])
        own[g][...] += ra[g][0].astype(F32) + ra[g][1].astype(F32)
        right, left = {a2: step(a2, 1)}, {a2: step(a2, -1)}
        for slot, by in enumerate((2, 1, -1)):
            t = step(a2, by)
            q[g][slot] = (own[g][:, t] if g == 1 else own[g][t]).astype(BF16)
        send((2, g, "x", 0), q[g].at[0, 0:2], rx2_[g].at[0], right)
        send((2, g, "x", 1), q[g].at[0, 2:4], rx2_[g].at[1], left)
        send((2, g, "a", 0, 1), q[g].at[1, 2:4], ra2_[g].at[0, 2:4], right)
        send((2, g, "a", 1, 0), q[g].at[2, 0:2], ra2_[g].at[1, 0:2], left)
    for g, (width, a1, a2, a3) in enumerate(GROUPS):
        right, left = {a2: step(a2, 1)}, {a2: step(a2, -1)}
        arrived((2, g, "x", 0), rx2_[g].at[0])
        q[g][1, 0:2] = (q[g][1, 0:2].astype(F32) + rx2_[g][0].astype(F32)).astype(BF16)
        arrived((2, g, "x", 1), rx2_[g].at[1])
        q[g][2, 2:4] = (q[g][2, 2:4].astype(F32) + rx2_[g][1].astype(F32)).astype(BF16)
        send((2, g, "a", 0, 0), q[g].at[1, 0:2], ra2_[g].at[0, 0:2], right)
        send((2, g, "a", 1, 1), q[g].at[2, 2:4], ra2_[g].at[1, 2:4], left)

    s = (s0, s1, s2)
    rx3 = (rx30, rx31, rx32)
    ra3 = (ra30, ra31, ra32)
    kept = []
    for g, (width, a1, a2, a3) in enumerate(GROUPS):
        for d in range(2):
            for h in range(2):
                arrived((2, g, "a", d, h), ra2_[g].at[d, h * 2:h * 2 + 2])
        mine = own[g].at[:, at[a2]] if g == 1 else own[g].at[at[a2]]
        mine[...] += ra2_[g][0].astype(F32) + ra2_[g][1].astype(F32)
        kept.append(mine)
        right, left = {a3: step(a3, 1)}, {a3: step(a3, -1)}
        for slot, by in enumerate((2, 1, -1)):
            s[g][slot] = mine[step(a3, by)].reshape(2, 16, width).astype(BF16)
        send((3, g, "x", 0), s[g].at[0, 0], rx3[g].at[0], right)
        send((3, g, "x", 1), s[g].at[0, 1], rx3[g].at[1], left)
        send((3, g, "a", 0, 1), s[g].at[1, 1], ra3[g].at[0, 1], right)
        send((3, g, "a", 1, 0), s[g].at[2, 0], ra3[g].at[1, 0], left)
    for g, (width, a1, a2, a3) in enumerate(GROUPS):
        right, left = {a3: step(a3, 1)}, {a3: step(a3, -1)}
        arrived((3, g, "x", 0), rx3[g].at[0])
        s[g][1, 0] = (s[g][1, 0].astype(F32) + rx3[g][0].astype(F32)).astype(BF16)
        arrived((3, g, "x", 1), rx3[g].at[1])
        s[g][2, 1] = (s[g][2, 1].astype(F32) + rx3[g][1].astype(F32)).astype(BF16)
        send((3, g, "a", 0, 0), s[g].at[1, 0], ra3[g].at[0, 0], right)
        send((3, g, "a", 1, 1), s[g].at[2, 1], ra3[g].at[1, 1], left)
    for g, (width, a1, a2, a3) in enumerate(GROUPS):
        for d in range(2):
            for h in range(2):
                arrived((3, g, "a", d, h), ra3[g].at[d, h])
        both = (ra3[g][0].astype(F32) + ra3[g][1].astype(F32)).reshape(32, width)
        fin_ref[ic, :, GOFF[g]:GOFF[g] + width] = kept[g][at[a3]] + both
    send(("fin",), fin_ref.at[ic], fin_ref.at[ic], mate)
    arrived(("fin",), fin_ref.at[other])

    both = fin_ref[...]
    tail = GTOT - 128
    gains = both[0, :, tail:] + both[1, :, tail:]
    body = both[:, :, :tail]
    squares = jnp.sum(jnp.sum(body * body, axis=0), axis=0, keepdims=True)
    row = sum(squares[:, n * 128:(n + 1) * 128] for n in range(10))
    ropes = jnp.where(lane == 32, 0.0, both[0, :, tail:] ** 2 + both[1, :, tail:] ** 2)
    ropes = ropes + jnp.where(lane == 32, gains * gains, 0.0)
    row = row + jnp.sum(ropes, axis=0, keepdims=True)
    row = jnp.broadcast_to(row, (8, 128))
    for n, axis in enumerate((AY, AX, AZ)):
        nbuf[n, 3] = row
        for m, by in enumerate((1, -1, 2)):
            send(("n", n, m), nbuf.at[n, 3], nbuf.at[n, m], {axis: step(axis, by)})
        for m in range(3):
            arrived(("n", n, m), nbuf.at[n, m])
        row = (nbuf[n, 0] + nbuf[n, 1]) + (nbuf[n, 2] + nbuf[n, 3])
    total = jnp.sum(row, axis=-1, keepdims=True)
    clip = jnp.minimum(1.0, lax.rsqrt(total / NPARAM + 1e-06))
    clip_ref[...] = jnp.broadcast_to(clip, (8, 128))

    for d in sends:
        d.wait_send()
    for d in tgd:
        d.wait()
    assert len(table) <= NSEM, len(table)


NSEM = 192


def scratch():
    v = pltpu.VMEM
    shapes = [
        v((512, 2048), BF16), v((512, 1024), BF16), v((512, 128), F32), v((512, 128), F32),
        v((4, 2, 8, 32, WCOL), BF16), v((4, 2, 8, 64, 256), BF16), v((4, 2, 8, 128), F32),
        v((2, 4, 4, 4, 32, 512), BF16), v((512, WCOL), F32),
        v((512, 512), BF16), v((512, 1024), BF16), v((512, 512), BF16), v((2, 512, 512), BF16),
        v((512, 512), F32), v((2, 512, 128), BF16), v((512, 128), F32),
        v((2, 512, 1024), BF16), v((512, 1024), BF16), v((2, 2, 512, 512), BF16), v((2, 512, 512), BF16),
        v((2, 512, 128), BF16), v((512, 128), BF16), v((512, 128), BF16), v((512, 128), F32),
        v((4, 4, 4, 32, 128), F32), v((8, 512, 256), BF16),
    ]
    ws = [w for w, *_ in GROUPS]
    shapes += [v((3, 4, 4, 32, w), BF16) for w in ws]
    shapes += [v((4, 4, 32, w), F32) for w in ws]
    shapes += [v((2, 2, 4, 32, w), BF16) for w in ws]
    shapes += [v((2, 4, 4, 32, w), BF16) for w in ws]
    shapes += [v((3, 4, 32, w), BF16) for w in ws]
    shapes += [v((2, 2, 32, w), BF16) for w in ws]
    shapes += [v((2, 4, 32, w), BF16) for w in ws]
    shapes += [v((3, 2, 16, w), BF16) for w in ws]
    shapes += [v((2, 16, w), BF16) for w in ws]
    shapes += [v((2, 2, 16, w), BF16) for w in ws]
    shapes += [v((3, 4, 8, 128), F32)]
    dma = pltpu.SemaphoreType.DMA
    return shapes + [dma((12,)), dma((NSEM,)), dma((NSEM,))]


def per_device(tokens, d_out, w_query, w_down, w_up, latent_gain):
    cosine, sine = rope_constants()
    vm = pl.BlockSpec(memory_space=pltpu.VMEM)
    anyspace = pl.BlockSpec(memory_space=pl.ANY)
    fin, clip, token_grad = pl.pallas_call(
        mega,
        out_shape=(
            jax.ShapeDtypeStruct((2, 32, GTOT), F32),
            jax.ShapeDtypeStruct((8, 128), F32),
            jax.ShapeDtypeStruct((SEQ, D), BF16),
        ),
        in_specs=[anyspace] * 4 + [vm] * 4,
        out_specs=(vm, vm, anyspace),
        scratch_shapes=scratch(),
        compiler_params=pltpu.CompilerParams(
            collective_id=0, has_side_effects=True, vmem_limit_bytes=67043328),
    )(tokens, d_out, jnp.asarray(cosine), jnp.asarray(sine), w_query, w_down, w_up,
      latent_gain.reshape(1, 64))
    ic = lax.axis_index(AC)
    clip = clip[0, 0]
    rows = lax.dynamic_slice_in_dim(fin, ic * 16, 16, 1)
    plain = jnp.concatenate([rows[0, :, :384], rows[0, :, 512:896], rows[0, :, 1024:1280]], 1)
    rest = jnp.concatenate([rows[1, :, :384], rows[1, :, 512:896], rows[1, :, 1024:1280]], 1)
    grad_query = jnp.concatenate(
        [plain.reshape(16, 8, 128), rest[:, :512].reshape(16, 8, 64)], -1).reshape(16, 1536)
    grad_down = jnp.concatenate([rest[:, 512:], rows[0, :, 1280:1312], rows[1, :, 1280:1312]], 1)
    up = jnp.stack([fin[:, :, 384:512], fin[:, :, 896:1024]], 2).reshape(2, 4, 8, 2, 128)
    up = lax.dynamic_slice_in_dim(up, ic * 4, 4, 2)
    grad_up = up.transpose(2, 0, 1, 3, 4).reshape(4, 2048)
    gain = lax.dynamic_slice_in_dim(fin[:, :, 1312], ic * 4, 4, 1)
    return (
        grad_query * clip,
        grad_down * clip,
        grad_up * clip,
        (gain[0] + gain[1]) * clip,
        token_grad,
    )


def solution(mesh):
    split = Mesh(mesh.devices.reshape(4, 4, 4, 2), NODE_LOCAL)
    return jax.shard_map(
        per_device,
        mesh=split,
        in_specs=(
            P(NODE_LOCAL, None),
            P(NODE_LOCAL, None),
            P(LOCAL, None),
            P(LOCAL, None),
            P(LOCAL, None),
            P(LOCAL),
        ),
        out_specs=(
            P(NODE_LOCAL, None),
            P(NODE_LOCAL, None),
            P(NODE_LOCAL, None),
            P(NODE_LOCAL),
            P(NODE_LOCAL, None),
        ),
        check_vma=False,
    )
```

time: 441 us -> 127 us (0.29)
  waiting for transfers between devices: 244 us -> 0 us
  Pallas kernels: 0 us -> 110 us
  matrix products: 84.2 us -> 0 us
  blocking collectives: 33.1 us -> 0 us
  other arithmetic: 29.2 us -> 3.95 us
  between operations: 16.8 us -> 0.68 us
  starting transfers between devices: 12.3 us -> 0 us
  local copies, waits for them, and re-layouts: 19.8 us -> 11.6 us
    reduce_scatter x2 -> x0, waiting for transfers between devices: 153 us -> none  [the longest x1 109 us: per_device(): lax.psum_scatter(lax.dot_general(tokens, joined, (((0,), (0,)), ((), ()))...]
    pallas_call x0 -> x1, Pallas kernels: none -> 110 us  [per_device(): pl.pallas_call(mega, out_shape=(jax.ShapeDtypeStruct((2, 32, GTOT), F32),...]
    dot_general x13 -> x0, matrix products: 84.2 us -> none  [the longest x3 17.8 us: transposed_product(): lax.dot_general(left, right, (((1,), (1,)), ((), ())), preferred_element_...]
    all_gather x2 -> x0, waiting for transfers between devices: 77.1 us -> none  [the longest x1 53.6 us: sent_together_2(): filled = lax.all_gather(both, axis, axis=dim, tiled=True)]
    psum x4 -> x0, blocking collectives: 33.1 us -> none  [one_axis_at_a_time(): shard = lax.psum(shard, axis)]
    all_to_all x2 -> x0, waiting for transfers between devices: 14.3 us -> none  [sum_at_owner(): pieces = lax.all_to_all(cut_along(shard, dim, size), axis, 0, 0, tiled=True)]
    all_to_all x2 -> x0, starting transfers between devices: 12.1 us -> none  [sum_at_owner(): pieces = lax.all_to_all(cut_along(shard, dim, size), axis, 0, 0, tiled=True)]
    concatenate x6 -> x1, other arithmetic: 10.1 us -> 0.01 us  [per_device(): jnp.concatenate([rows[1, :, :384], rows[1, :, 512:896], rows[1, :, 1024:1...]
  transfers between devices with their start and end apart: 6 -> 0, of which waited for: 5 -> 0; matrix products, arithmetic and copies ran while one was open for 10% -> 0% of each run, Pallas kernels for 0% -> 0%
where the time goes in v1:
time: 127 us; the launch traced here: 126 us
  Pallas kernels  110 us (87%)
  local copies, waits for them, and re-layouts  11.6 us (9%)
  other arithmetic  3.95 us (3%)
    pallas_call x1, Pallas kernels, per_device(): pl.pallas_call(mega, out_shape=(jax.ShapeDtypeStruct((2, 32, GTOT), F32),...  110 us
    unnamed x3, local copies, waits for them, and re-layouts  5.03 us

profile of v1, /device:TPU:1, one launch (start us, length us, event | category | flops | bytes accessed | tf_op | source)
XLA Modules:
  0.0 126.0 jit_solution(5756871532196104675)
XLA Ops:
  0.6 1.9 %copy.15.wd_ref = bf16[256,576]{1,0:T(8,128)(2,1)} copy(bf16[256,576]{0,1:T(8,128)(2,1)} %param.11) | data formatting | bytes 589824 | tf_op args[3]
  2.5 109.8 %shard_map.119 = (f32[2,32,1408]{2,1,0:T(8,128)}, f32[8,128]{1,0:T(8,128)}, bf16[512,2048]{1,0:T(8,128)(2,1)}) custom-call(bf16[512,2048]{1,0:T(8,128)(2,1)} %tokens_hbm.1, bf16[512,1024]{1,0:T(8,128)(2,1)} %dout_hbm.1, f32[512,128]{1,0:T(8,128)} %constant.19.clone.cos_hbm, f32[512,128]{1,0:T(8,128)} %constant.20.clone.sin_hbm, bf16[256,1536]{1,0:T(8,128)(2,1)} %wq_ref.1, ...), custom_call_target="tpu_custom_call" | custom-call | tf_op jit(solution)/shard_map/pallas_call | solution.py:577
  112.3 1.2 slice.58
  113.5 0.7 dynamic-slice_bitcast_fusion.7
  114.2 0.7 dynamic-slice_bitcast_fusion.4
  115.0 0.8 slice.65
  115.8 1.3 %fusion.8 = f32[4]{0:T(128)} fusion(f32[2,32,1]{2,1,0:T(8,128)S(1)} %slice.65, s32[]{:T(128)S(6)} %add.20, s32[]{:T(128)S(6)} %select_n.11, f32[]{:T(128)} %bitcast.6), kind=kLoop, calls=%fused_computation.26 | loop fusion | flops 8 | bytes 60 | tf_op jit(solution)/shard_map/mul | solution.py:607
  117.1 0.8 slice_bitcast_fusion
  117.9 0.8 dynamic-slice_bitcast_fusion.3
  118.7 0.7 fusion.5
  119.4 0.6 mul.53
  120.1 1.3 %fusion.2 = f32[16,576]{1,0:T(8,128)} fusion(f32[16,256]{1,0:T(8,128)S(1)} %get-tuple-element.15, f32[16,384]{1,0:T(8,128)S(1)} %get-tuple-element.18, f32[16,32]{1,0:T(8,128)S(1)} %get-tuple-element.14, f32[16,32]{1,0:T(8,128)S(1)} %get-tuple-element.13, f32[]{:T(128)} %bitcast.6), kind=kLoop, calls=%fused_computation.7 | loop fusion | flops 36864 | bytes 81924 | tf_op jit(solution)/shard_map/mul | solution.py:605
  121.4 0.1 reshape.40
  121.5 0.7 maximum_multiply_fusion
  122.1 0.7 mul.46
  122.9 3.2 %copy.19 = bf16[512,2048]{1,0:T(8,128)(2,1)} copy(bf16[512,2048]{1,0:T(8,128)(2,1)} %get-tuple-element.30) | data formatting | bytes 4194304
  (4 shorter events, 0.1 us)

commit v2 on v1

v2 whole, which is shorter than its diff:
```python
import math

import jax
import jax.numpy as jnp
import numpy as np
from jax import lax
from jax.experimental import pallas as pl
from jax.experimental.pallas import tpu as pltpu
from jax.sharding import Mesh
from jax.sharding import PartitionSpec as P

H = 8
DN = 128
DR = 64
DV = 128
KVL = 512
SEQ = 512
D = 2048
NPARAM = 5374464
EPSILON = 1e-06
ROPE_BASE = 10000.0
LOCAL = ("local_0", "local_1")
NODE_LOCAL = ("node_0", "node_1", "local_0", "local_1")
MESH = pl.DeviceIdType.MESH
AZ, AX, AY, AC = NODE_LOCAL

WCOL = 2176
SUBS = ((0, 640), (640, 1408), (1408, 2176))
SCALE = 1.0 / math.sqrt(DN + DR)
AXES = ((AZ, AX, AY), (AX, AY, AZ), (AY, AZ, AX))
UNITS = tuple((w,) + AXES[n % 3] for n, w in enumerate((256, 256, 256, 256, 256, 128)))
GOFF = (0, 256, 512, 768, 1024, 1280)
GTOT = 1408
F32 = jnp.float32
BF16 = jnp.bfloat16


def rope_constants():
    position = np.arange(SEQ, dtype=np.float32)[:, None]
    freq = np.float32(ROPE_BASE) ** (-np.arange(DR // 2, dtype=np.float32) * np.float32(2.0 / DR))
    angle = (position * freq[None, :].astype(np.float32)).astype(np.float32)
    cosine = np.cos(angle).astype(np.float32)
    sine = np.sin(angle).astype(np.float32)
    return np.concatenate([cosine] * 4, 1), np.concatenate([-sine, sine] * 2, 1)


def nt(a, b):
    return lax.dot_general(a, b, (((1,), (1,)), ((), ())), preferred_element_type=F32)


def nn(a, b):
    return jnp.dot(a, b, preferred_element_type=F32)


def tn(a, b):
    return lax.dot_general(a, b, (((0,), (0,)), ((), ())), preferred_element_type=F32)


def mega(
    tokens_hbm, dout_hbm, cos_hbm, sin_hbm, wq_ref, wd_ref, wu_ref, gain_ref,
    fin_ref, clip_ref, tg_hbm,
    tokens, dout, cosr, sinr, wbuf, ubuf, gbuf, tokt, acc, qrope, qnope, nrm, nrt, ng, krp, dkr,
    jb, jp, kvg, kvgp, rg, rgp, rgf, invr, gmat, tgb, nbuf, lsem, ssem, rsem, *rest,
):
    nu = len(UNITS)
    part, own, rx, ra, part2, rx2, ra2, part3, ra3 = (rest[n * nu:(n + 1) * nu] for n in range(9))
    iz, ix, iy, ic = (lax.axis_index(a) for a in NODE_LOCAL)
    at = {AZ: iz, AX: ix, AY: iy}
    other = 1 - ic
    STEP = {(a, by): lax.rem(at[a] + (by + 4), 4) for a in at for by in (-1, 0, 1, 2)}

    def step(axis, by):
        return STEP[axis, by]

    sends = []
    table = {}
    scope = []

    def mark(name):
        while scope:
            scope.pop().__exit__(None, None, None)
        if name:
            scope.append(jax.named_scope(name))
            scope[-1].__enter__()

    mark("start")

    def sem_of(key):
        return table.setdefault(key, len(table))

    def send(key, src, dst, peer):
        k = sem_of(key)
        d = pltpu.make_async_remote_copy(
            src_ref=src, dst_ref=dst, send_sem=ssem.at[k], recv_sem=rsem.at[k],
            device_id=peer, device_id_type=MESH)
        d.start()
        sends.append((k, src, dst, peer))

    def arrived(key, dst):
        k = sem_of(key)
        pltpu.make_async_remote_copy(
            src_ref=dst, dst_ref=dst, send_sem=ssem.at[k], recv_sem=rsem.at[k],
            device_id=mate, device_id_type=MESH).wait_recv()

    mate = {AC: other}
    locals_ = []
    for n, (src, dst) in enumerate(((tokens_hbm, tokens), (dout_hbm, dout), (cos_hbm, cosr), (sin_hbm, sinr))):
        d = pltpu.make_async_copy(src, dst, lsem.at[n])
        d.start()
        locals_.append(d)

    barrier = pltpu.get_barrier_semaphore()
    for axis in (AZ, AX, AY):
        for by in (1, -1, 2):
            pl.semaphore_signal(barrier, inc=1, device_id={axis: step(axis, by)}, device_id_type=MESH)
    pl.semaphore_signal(barrier, inc=1, device_id=mate, device_id_type=MESH)

    down = jnp.concatenate([wd_ref[...], jnp.zeros((64, 256), BF16)], 0)
    wbuf[iy, ic, :, :, 0:640] = down.T.reshape(8, 32, 640)
    for n in range(4):
        lo = 640 + n * 384
        h = n * 384
        both = jnp.concatenate([
            wq_ref[:, h:h + 128], wq_ref[:, h + 192:h + 320],
            wq_ref[:, h + 128:h + 192], wq_ref[:, h + 320:h + 384]], 1)
        wbuf[iy, ic, :, :, lo:lo + 384] = both.reshape(8, 32, 384)
    for p in range(8):
        ubuf[iy, ic, p] = wu_ref[:, p * 256:(p + 1) * 256]
    gbuf[iy, ic] = jnp.broadcast_to(
        jnp.concatenate([gain_ref[...].astype(F32), jnp.zeros((1, 64), F32)], 1), (8, 128))
    pl.semaphore_wait(barrier, 10)

    RING = (AX, AZ)
    YO = (step(AY, -1), step(AY, 1), step(AY, 2))
    PIECE = {(k, by): k * 4 + step(RING[k], by) for k in range(2) for by in (-1, 0, 1, 2)}
    KINDS = (0, "u", 1, 2)

    def block_of(kind, yy, core):
        if kind == "u":
            return ubuf.at[yy, core]
        lo, hi = SUBS[kind]
        return wbuf.at[yy, core, :, :, lo:hi]

    def piece(kind, yy, k, by):
        if kind == "u":
            return ubuf.at[yy, ic, PIECE[k, by]]
        lo, hi = SUBS[kind]
        return wbuf.at[yy, ic, PIECE[k, by], :, lo:hi]

    def half_piece(kind, yy, k, by, d):
        if kind == "u":
            return ubuf.at[yy, ic, PIECE[k, by], d * 32:d * 32 + 32]
        lo, hi = SUBS[kind]
        return wbuf.at[yy, ic, PIECE[k, by], d * 16:d * 16 + 16, lo:hi]

    def y_send(kind):
        for k in range(2):
            r = piece(kind, iy, k, 0)
            send((kind, "y", k, 0), r, r, {AY: step(AY, 1)})
            send((kind, "y", k, 1), r, r, {AY: step(AY, -1)})

    def p_send(kind, k, yo):
        r = piece(kind, YO[yo], k, 0)
        send((kind, "p", k, yo, 0), r, r, {RING[k]: step(RING[k], 1)})
        send((kind, "p", k, yo, 1), r, r, {RING[k]: step(RING[k], -1)})

    def y_take(kind):
        for k in range(2):
            for d in range(2):
                arrived((kind, "y", k, d), piece(kind, YO[d], k, 0))
                half = half_piece(kind, YO[d], k, 0, d)
                send((kind, "y2", k, d), half, half, {AY: step(AY, 1 if d == 0 else -1)})
                p_send(kind, k, d)

    def y2_take(kind):
        for k in range(2):
            for d in range(2):
                arrived((kind, "y2", k, d), half_piece(kind, YO[2], k, 0, d))
            p_send(kind, k, 2)

    def p_take(kind, yo):
        for k in range(2):
            for d in range(2):
                by = -1 if d == 0 else 1
                arrived((kind, "p", k, yo, d), piece(kind, YO[yo], k, by))
                half = half_piece(kind, YO[yo], k, by, d)
                send((kind, "p2", k, yo, d), half, half, {RING[k]: step(RING[k], -by)})

    def p2_take(kind, yo):
        for k in range(2):
            for d in range(2):
                arrived((kind, "p2", k, yo, d), half_piece(kind, YO[yo], k, 2, d))
        to_mate(kind, yo)

    def to_mate(kind, yo):
        r = block_of(kind, iy if yo is None else YO[yo], ic)
        send((kind, "d", yo), r, r, mate)

    def from_mate(kind):
        for yo in (None, 0, 1, 2):
            arrived((kind, "d", yo), block_of(kind, iy if yo is None else YO[yo], other))

    def project(lo, hi):
        return nn(tokens[...], wbuf[:, :, :, :, lo:hi].reshape(2048, hi - lo))

    mark("gather")
    y_send(0)
    y_send("u")
    to_mate(0, None)
    g = gbuf.at[iy, ic]
    for n, by in enumerate((1, -1, 2)):
        send(("g", n), g, g, {AY: step(AY, by)})
    send(("gd", 3), g, g, mate)
    to_mate("u", None)
    mark("y0")
    y_take(0)
    y_send(1)
    to_mate(1, None)
    mark("yu")
    y_take("u")
    locals_[0].wait()
    mark("transpose")
    for z in range(2):
        tokt[0, z] = tokens[:, z * 512:(z + 1) * 512].T.reshape(4, 4, 32, 512)
    mark("y20")
    y2_take(0)
    y_send(2)
    to_mate(2, None)
    mark("p0a")
    p_take(0, 0)
    p_take(0, 1)
    mark("y1")
    y_take(1)
    mark("transpose")
    for z in range(2, 4):
        tokt[0, z] = tokens[:, z * 512:(z + 1) * 512].T.reshape(4, 4, 32, 512)
    send(("tok",), tokt.at[0], tokt.at[1], mate)
    mark("y2u")
    y2_take("u")
    mark("pua")
    p_take("u", 0)
    p_take("u", 1)
    mark("p0b")
    p_take(0, 2)
    mark("y21")
    y2_take(1)
    mark("p20")
    p2_take(0, 0)
    p2_take(0, 1)
    mark("y2")
    y_take(2)
    mark("p1a")
    p_take(1, 0)
    p_take(1, 1)
    mark("pub")
    p_take("u", 2)
    mark("p202")
    p2_take(0, 2)
    mark("y22")
    y2_take(2)
    mark("g")
    for n, by in enumerate((-1, 1, 2)):
        gg = gbuf.at[step(AY, by), ic]
        arrived(("g", n), gg)
        send(("gd", n), gg, gg, mate)
    mark("p2u")
    for yo in range(3):
        p2_take("u", yo)
    mark("p1b")
    p_take(1, 2)
    mark("p21")
    p2_take(1, 0)
    p2_take(1, 1)
    mark("p2a")
    p_take(2, 0)
    p_take(2, 1)
    mark("down")
    from_mate(0)
    acc[...] = project(*SUBS[0])
    mark("p212")
    p2_take(1, 2)
    mark("pre")
    for n, by in enumerate((-1, 1, 2)):
        arrived(("gd", n), gbuf.at[step(AY, by), other])
    arrived(("gd", 3), gbuf.at[iy, other])

    for d in locals_[1:]:
        d.wait()

    lane = lax.broadcasted_iota(jnp.int32, (1, 128), 1)
    low = lax.rem(lane, 64) < 32

    def swap(v):
        return jnp.where(low, pltpu.roll(v, 96, 1), pltpu.roll(v, 32, 1))

    def rot(v, sign):
        return v * cosr[...] + swap(v) * (sinr[...] * sign)

    gain = jnp.concatenate([gbuf[y, c, 0:1, 0:64] for y in range(4) for c in range(2)], 1)
    kr = rot(acc[:, 512:640], 1.0)
    krp[0] = jnp.where(lane < 64, kr, 0.0).astype(BF16)
    krp[1] = jnp.where(lane < 64, 0.0, pltpu.roll(kr, 64, 1)).astype(BF16)
    for n in range(4):
        rows = slice(n * 128, (n + 1) * 128)
        latent = acc[rows, 0:512]
        inv = lax.rsqrt(jnp.mean(latent * latent, axis=-1, keepdims=True) + EPSILON)
        unit = latent * inv
        acc[rows, 0:512] = unit
        invr[rows] = jnp.broadcast_to(inv, (128, 128))
        nrm[rows] = (unit * gain).astype(BF16)
    nrt[0] = nrm[...].T
    send(("nrt",), nrt.at[0], nrt.at[1], mate)
    ng[...] = jnp.zeros((512, 512), F32)
    dkr[...] = jnp.zeros((512, 128), F32)
    mark("p2b")
    p_take(2, 2)
    from_mate("u")
    mark("heads")

    tri = (lax.broadcasted_iota(jnp.int32, (256, 256), 0)
           <= lax.broadcasted_iota(jnp.int32, (256, 256), 1))

    def block(kf, v, qf, do):
        rows = kf.shape[0]
        s = nt(kf, qf) * SCALE
        masked = jnp.where(tri, s[rows - 256:], -1e30)
        s = masked if rows == 256 else jnp.concatenate([s[:rows - 256], masked], 0)
        w = jnp.exp(s - jnp.max(s, axis=0, keepdims=True))
        probs = w * (1.0 / jnp.sum(w, axis=0, keepdims=True))
        dp = nt(v, do)
        delta = jnp.sum(probs * dp, axis=0, keepdims=True)
        ds = (probs * (dp - delta) * SCALE).astype(BF16)
        return probs.astype(BF16), ds

    def queries(s):
        from_mate(s + 1)
        lo = SUBS[s + 1][0]
        q = project(lo, lo + 768)
        for m in range(2):
            n = 2 * s + m
            qnope[:, n * 256:(n + 1) * 256] = q[:, m * 384:m * 384 + 256].astype(BF16)
            rope = q[:, m * 384 + 256:m * 384 + 384].astype(BF16).astype(F32)
            qrope[:, n * 128:(n + 1) * 128] = rot(rope, 1.0).astype(BF16)

    def pair(n, carry):
        @pl.when(n == 0)
        def _():
            queries(0)

        @pl.when(n == 1)
        def _():
            p2_take(2, 0)
            p2_take(2, 1)
            p2_take(2, 2)

        @pl.when(n == 2)
        def _():
            queries(1)

        half, m = n // 2, lax.rem(n, 2)
        qr = qrope[:, pl.ds(pl.multiple_of(n * 128, 128), 128)]
        total = None
        for e in range(2):
            h = 2 * n + e
            hc = pl.ds(pl.multiple_of(h * 128, 128), 128)
            jc = pl.ds(pl.multiple_of((m * 2 + e) * 128, 128), 128)
            u = ubuf[:, :, h].reshape(512, 256)
            kv = nn(nrm[...], u).astype(BF16)
            kf = jnp.concatenate([kv[:, :128], krp[e]], 1)
            v = kv[:, 128:]
            qf = jnp.concatenate([qnope[:, hc], qr], 1)
            do = dout[:, hc]
            pa, da = block(kf[:256], v[:256], qf[:256], do[:256])
            pb, db = block(kf, v, qf[256:], do[256:])
            dv = nn(pb, do[256:])
            dv = jnp.concatenate([dv[:256] + nn(pa, do[:256]), dv[256:]], 0)
            dk = nn(db, qf[256:])
            dk = jnp.concatenate([dk[:256] + nn(da, qf[:256]), dk[256:]], 0)
            dq = jnp.concatenate([tn(da, kf[:256]), tn(db, kf)], 0)
            jb[half, :, jc] = dq[:, :128].astype(BF16)
            total = dq[:, 128:] if e == 0 else total + dq[:, 128:]
            keep = lane < 64 if e == 0 else lane >= 64
            dkr[...] += jnp.where(keep, dk[:, 128:], 0.0)
            kg = dk[:, :128].astype(BF16)
            vg = dv.astype(BF16)
            kvg[half, 0, :, jc] = kg
            kvg[half, 1, :, jc] = vg
            ng[...] += nt(jnp.concatenate([kg, vg], 1), u)
        jb[half, :, pl.ds(pl.multiple_of(512 + m * 128, 128), 128)] = rot(total, -1.0).astype(BF16)
        return carry

    lax.fori_loop(0, 4, pair, 0)
    mark("post")
    send(("j",), jb.at[other, :, 0:768], jp.at[:, 0:768], mate)

    gterm = jnp.zeros((1, 512), F32)
    for n in range(4):
        rows = slice(n * 128, (n + 1) * 128)
        unit = acc[rows, 0:512]
        grad = ng[rows]
        gterm = gterm + jnp.sum(grad * unit, axis=0, keepdims=True)
        scaled = grad * gain
        inner = jnp.mean(scaled * unit, axis=-1, keepdims=True)
        value = (invr[rows, 0:1] * (scaled - unit * inner)).astype(BF16)
        jb[0, rows, 768:1024] = value[:, :256]
        jb[1, rows, 768:1024] = value[:, 256:]
    dk = dkr[...]
    rope = jnp.where(lane < 64, rot(dk + pltpu.roll(dk, 64, 1), -1.0), 0.0)
    rgf[...] = rope.astype(BF16)
    rg[0] = jnp.where(lane < 32, rope, 0.0).astype(BF16)
    rg[1] = jnp.where(lane < 32, pltpu.roll(rope, 96, 1), 0.0).astype(BF16)
    send(("kvg",), kvg.at[other], kvgp, mate)
    send(("jl",), jb.at[other, :, 768:1024], jp.at[:, 768:1024], mate)
    send(("rg",), rg.at[other], rgp, mate)
    column = jnp.broadcast_to(gterm, (128, 512)).T
    column = jnp.where(lane == 32, column, 0.0).reshape(64, 8, 128)
    gmat[...] = jnp.concatenate([column, jnp.zeros((64, 24, 128), F32)], 1).reshape(4, 4, 4, 32, 128)

    tgd = []

    def token_block():
        n = len(tgd)
        w = wbuf[n // 2, n % 2].reshape(256, WCOL)
        cols = [jb[0, :, 768:], jb[1, :, 768:], rgf[...]]
        for m in range(4):
            cols += [jb[m // 2, :, m % 2 * 256:m % 2 * 256 + 256],
                     jb[m // 2, :, 512 + m % 2 * 128:640 + m % 2 * 128]]
        tgb[n] = nt(jnp.concatenate(cols, 1), w).astype(BF16)
        d = pltpu.make_async_copy(tgb.at[n], tg_hbm.at[:, n * 256:(n + 1) * 256], lsem.at[4 + n])
        d.start()
        tgd.append(d)

    mark("waitmate")
    arrived(("tok",), tokt.at[1])
    arrived(("nrt",), nrt.at[1])
    arrived(("j",), jp.at[:, 0:768])

    def chunk(u, t):
        g = u % 3
        lo, width = (g * 256, 256) if u < 3 else (768 + g * 128, 128)
        total = None
        for n in range(2):
            src = (tokt.at[n, t], tokt.at[n, :, t], tokt.at[n, :, :, t])[g]
            left = src[...].reshape(512, 512)
            if u == 5:
                right = rg[ic] if n == 0 else rgp[...]
            else:
                right = jb[ic, :, lo:lo + width] if n == 0 else jp[:, lo:lo + width]
            term = nn(left, right)
            total = term if n == 0 else total + term
        total = total.reshape(4, 4, 32, width)
        if u < 3:
            return total
        if u == 5:
            return total + gmat[:, :, t]
        up = None
        for n in range(2):
            if g == 0:
                left = nrt[n, pl.ds(pl.multiple_of(t * 128, 128), 128)]
            else:
                left = jnp.concatenate(
                    [nrt[n, pl.ds(pl.multiple_of(z * 128 + t * 32, 32), 32)] for z in range(4)], 0)
            term = nn(left, kvg[ic, g] if n == 0 else kvgp[g])
            up = term if n == 0 else up + term
        up = up.reshape(16, 8, 512)
        up = jnp.concatenate([up[:, :, j * 128:(j + 1) * 128] for j in range(4)], 1)
        return jnp.concatenate([total, up.reshape(4, 4, 32, 128)], -1)

    def ways(axis):
        return {axis: step(axis, 1)}, {axis: step(axis, -1)}

    def first_sends(us):
        for slot, by in enumerate((2, 1, -1)):
            for u in us:
                right, left = ways(UNITS[u][1])
                part[u][slot] = chunk(u, step(UNITS[u][1], by)).astype(BF16)
                if by == 2:
                    send((1, u, "x", 0), part[u].at[0, 0:2], rx[u].at[0], right)
                    send((1, u, "x", 1), part[u].at[0, 2:4], rx[u].at[1], left)
                elif by == 1:
                    send((1, u, "a", 0, 1), part[u].at[1, 2:4], ra[u].at[0, 2:4], right)
                else:
                    send((1, u, "a", 1, 0), part[u].at[2, 0:2], ra[u].at[1, 0:2], left)

    def relay(phase, us, p, r, a):
        for u in us:
            right, left = ways(UNITS[u][phase])
            arrived((phase, u, "x", 0), r[u].at[0])
            p[u][1, 0:2] = (p[u][1, 0:2].astype(F32) + r[u][0].astype(F32)).astype(BF16)
            arrived((phase, u, "x", 1), r[u].at[1])
            p[u][2, 2:4] = (p[u][2, 2:4].astype(F32) + r[u][1].astype(F32)).astype(BF16)
            send((phase, u, "a", 0, 0), p[u].at[1, 0:2], a[u].at[0, 0:2], right)
            send((phase, u, "a", 1, 1), p[u].at[2, 2:4], a[u].at[1, 2:4], left)

    def own_chunks(us):
        for u in us:
            own[u][...] = chunk(u, at[UNITS[u][1]])

    def settle(phase, u, a):
        for d in range(2):
            for h in range(2):
                arrived((phase, u, "a", d, h), a[u].at[d, h * 2:h * 2 + 2])

    def second(u, t):
        return own[u].at[:, t] if u % 3 == 1 else own[u].at[t]

    def second_sends(us):
        for u in us:
            settle(1, u, ra)
            own[u][...] += ra[u][0].astype(F32) + ra[u][1].astype(F32)
            right, left = ways(UNITS[u][2])
            for slot, by in enumerate((2, 1, -1)):
                part2[u][slot] = second(u, step(UNITS[u][2], by))[...].astype(BF16)
            send((2, u, "x", 0), part2[u].at[0, 0:2], rx2[u].at[0], right)
            send((2, u, "x", 1), part2[u].at[0, 2:4], rx2[u].at[1], left)
            send((2, u, "a", 0, 1), part2[u].at[1, 2:4], ra2[u].at[0, 2:4], right)
            send((2, u, "a", 1, 0), part2[u].at[2, 0:2], ra2[u].at[1, 0:2], left)

    def third_sends(us):
        for u in us:
            settle(2, u, ra2)
            mine = second(u, at[UNITS[u][2]])
            mine[...] += ra2[u][0].astype(F32) + ra2[u][1].astype(F32)
            for slot, by in enumerate((2, 1, -1)):
                part3[u][slot] = mine[step(UNITS[u][3], by)].astype(BF16)
                send((3, u, slot), part3[u].at[slot], ra3[u].at[slot], {UNITS[u][3]: step(UNITS[u][3], by)})

    def last_sums(us):
        for u in us:
            for slot in range(3):
                arrived((3, u, slot), ra3[u].at[slot])
            mine = second(u, at[UNITS[u][2]])[at[UNITS[u][3]]]
            fin_ref[ic, :, GOFF[u]:GOFF[u] + UNITS[u][0]] = mine + (
                ra3[u][0].astype(F32) + ra3[u][1].astype(F32) + ra3[u][2].astype(F32))

    A, B = (0, 1, 2), (3, 4, 5)
    mark("firstA")
    first_sends(A)
    mark("relayA")
    relay(1, A, part, rx, ra)
    mark("mateB")
    arrived(("kvg",), kvgp)
    arrived(("jl",), jp.at[:, 768:1024])
    arrived(("rg",), rgp)
    mark("firstB")
    first_sends(B)
    mark("relayB")
    relay(1, B, part, rx, ra)
    mark("ownA")
    own_chunks(A)
    mark("secondA")
    second_sends(A)
    mark("ownB")
    own_chunks(B)
    mark("tg")
    for n in range(3):
        token_block()
    mark("relay2A")
    relay(2, A, part2, rx2, ra2)
    mark("tg")
    for n in range(2):
        token_block()
    mark("secondB")
    second_sends(B)
    mark("thirdA")
    third_sends(A)
    mark("tg")
    for n in range(1):
        token_block()
    mark("relay2B")
    relay(2, B, part2, rx2, ra2)
    mark("tg")
    for n in range(2):
        token_block()
    mark("lastA")
    last_sums(A)
    send(("fin", 0), fin_ref.at[ic, :, 0:768], fin_ref.at[ic, :, 0:768], mate)
    mark("thirdB")
    third_sends(B)
    mark("lastB")
    last_sums(B)
    send(("fin", 1), fin_ref.at[ic, :, 768:GTOT], fin_ref.at[ic, :, 768:GTOT], mate)
    mark("fin")
    arrived(("fin", 0), fin_ref.at[other, :, 0:768])
    arrived(("fin", 1), fin_ref.at[other, :, 768:GTOT])

    both = fin_ref[...]
    tail = GTOT - 128
    gains = both[0, :, tail:] + both[1, :, tail:]
    body = both[:, :, :tail]
    squares = jnp.sum(jnp.sum(body * body, axis=0), axis=0, keepdims=True)
    row = sum(squares[:, n * 128:(n + 1) * 128] for n in range(10))
    ropes = jnp.where(lane == 32, 0.0, both[0, :, tail:] ** 2 + both[1, :, tail:] ** 2)
    ropes = ropes + jnp.where(lane == 32, gains * gains, 0.0)
    row = row + jnp.sum(ropes, axis=0, keepdims=True)
    row = jnp.broadcast_to(row, (8, 128))
    mark("norm")
    for n, axis in enumerate((AY, AX, AZ)):
        nbuf[n, 3] = row
        for m, by in enumerate((1, -1, 2)):
            send(("n", n, m), nbuf.at[n, 3], nbuf.at[n, m], {axis: step(axis, by)})
        for m in range(3):
            arrived(("n", n, m), nbuf.at[n, m])
        row = (nbuf[n, 0] + nbuf[n, 1]) + (nbuf[n, 2] + nbuf[n, 3])
    total = jnp.sum(row, axis=-1, keepdims=True)
    clip = jnp.minimum(1.0, lax.rsqrt(total / NPARAM + 1e-06))
    clip_ref[...] = jnp.broadcast_to(clip, (8, 128))

    mark("drain")
    for k, src, dst, peer in sends:
        pltpu.make_async_remote_copy(
            src_ref=src, dst_ref=dst, send_sem=ssem.at[k], recv_sem=rsem.at[k],
            device_id=peer, device_id_type=MESH).wait_send()
    for d in tgd:
        d.wait()
    mark(None)
    assert len(table) <= NSEM, len(table)


NSEM = 280


def scratch():
    v = pltpu.VMEM
    dma = pltpu.SemaphoreType.DMA
    shapes = [
        v((512, 2048), BF16), v((512, 1024), BF16), v((512, 128), F32), v((512, 128), F32),
        v((4, 2, 8, 32, WCOL), BF16), v((4, 2, 8, 64, 256), BF16), v((4, 2, 8, 128), F32),
        v((2, 4, 4, 4, 32, 512), BF16), v((512, 640), F32),
        v((512, 512), BF16), v((512, 1024), BF16), v((512, 512), BF16), v((2, 512, 512), BF16),
        v((512, 512), F32), v((2, 512, 128), BF16), v((512, 128), F32),
        v((2, 512, 1024), BF16), v((512, 1024), BF16), v((2, 2, 512, 512), BF16), v((2, 512, 512), BF16),
        v((2, 512, 128), BF16), v((512, 128), BF16), v((512, 128), BF16), v((512, 128), F32),
        v((4, 4, 4, 32, 128), F32), v((8, 512, 256), BF16), v((3, 4, 8, 128), F32),
        dma((12,)), dma((NSEM,)), dma((NSEM,)),
    ]
    ws = [w for w, *_ in UNITS]
    shapes += [v((3, 4, 4, 32, w), BF16) for w in ws]
    shapes += [v((4, 4, 32, w), F32) for w in ws]
    shapes += [v((2, 2, 4, 32, w), BF16) for w in ws]
    shapes += [v((2, 4, 4, 32, w), BF16) for w in ws]
    shapes += [v((3, 4, 32, w), BF16) for w in ws]
    shapes += [v((2, 2, 32, w), BF16) for w in ws]
    shapes += [v((2, 4, 32, w), BF16) for w in ws]
    shapes += [v((3, 32, w), BF16) for w in ws]
    shapes += [v((3, 32, w), BF16) for w in ws]
    return shapes


def last_step(fin_ref, clip_ref, tg_in, gq_ref, gd_ref, gu_ref, gg_ref, tg_out, stage, isem, osem):
    ic = lax.axis_index(AC)
    reads = []
    for n in range(4):
        rows = slice(n * 128, (n + 1) * 128)
        d = pltpu.make_async_copy(tg_in.at[rows], stage.at[n], isem.at[n])
        d.start()
        reads.append(d)
    clip = clip_ref[0:1, 0:1]
    first = ic == 0

    def rows(half, cols):
        return jnp.where(first, fin_ref[half, 0:16, cols], fin_ref[half, 16:32, cols]) * clip

    def cols(lo):
        return slice(lo, lo + 128)

    for n in range(4):
        half, m = n // 2, n % 2
        rope = rows(half, cols(512 + m * 128))
        gq_ref[:, n * 384:(n + 1) * 384] = jnp.concatenate(
            [rows(half, cols(m * 256)), rope[:, :64], rows(half, cols(m * 256 + 128)), rope[:, 64:]], 1)
        gd_ref[:, n * 128:(n + 1) * 128] = rows(half, cols(768 + m * 256))
    tail = slice(GTOT - 128, GTOT)
    gd_ref[:, 512:576] = jnp.concatenate([rows(0, tail)[:, :32], rows(1, tail)[:, :32]], 1)
    for h in range(H):
        half, j = h // 4, h % 4
        for u in range(2):
            block = fin_ref[half, j * 8:j * 8 + 8, cols(896 + u * 256)] * clip
            gu_ref[:, h * 256 + u * 128:h * 256 + u * 128 + 128] = jnp.where(first, block[0:4], block[4:8])
    gain = (fin_ref[0, 0:8, tail] + fin_ref[1, 0:8, tail]) * clip
    gain = jnp.where(first, gain[0:4], gain[4:8])
    spread = (lax.broadcasted_iota(jnp.int32, (4, 128), 0)
              == lax.broadcasted_iota(jnp.int32, (4, 128), 1))
    gg_ref[...] = jnp.sum(jnp.where(spread, gain[:, 32:33], 0.0), axis=0)[0:4]
    writes = []
    for n in range(4):
        rows_n = slice(n * 128, (n + 1) * 128)
        reads[n].wait()
        d = pltpu.make_async_copy(stage.at[n], tg_out.at[rows_n], osem.at[n])
        d.start()
        writes.append(d)
    for d in writes:
        d.wait()


def finish(fin, clip, token_grad):
    vm = pl.BlockSpec(memory_space=pltpu.VMEM)
    anyspace = pl.BlockSpec(memory_space=pl.ANY)
    return pl.pallas_call(
        last_step,
        out_shape=(
            jax.ShapeDtypeStruct((16, 1536), F32),
            jax.ShapeDtypeStruct((16, 576), F32),
            jax.ShapeDtypeStruct((4, 2048), F32),
            jax.ShapeDtypeStruct((4,), F32),
            jax.ShapeDtypeStruct((SEQ, D), BF16),
        ),
        in_specs=[vm, vm, anyspace],
        out_specs=(vm, vm, vm, vm, anyspace),
        scratch_shapes=[
            pltpu.VMEM((4, 128, D), BF16), pltpu.SemaphoreType.DMA((4,)), pltpu.SemaphoreType.DMA((4,))],
    )(fin, clip, token_grad)


def per_device(tokens, d_out, w_query, w_down, w_up, latent_gain):
    cosine, sine = rope_constants()
    vm = pl.BlockSpec(memory_space=pltpu.VMEM)
    anyspace = pl.BlockSpec(memory_space=pl.ANY)
    fin, clip, token_grad = pl.pallas_call(
        mega,
        out_shape=(
            jax.ShapeDtypeStruct((2, 32, GTOT), F32),
            jax.ShapeDtypeStruct((8, 128), F32),
            jax.ShapeDtypeStruct((SEQ, D), BF16),
        ),
        in_specs=[anyspace] * 4 + [vm] * 4,
        out_specs=(vm, vm, anyspace),
        scratch_shapes=scratch(),
        compiler_params=pltpu.CompilerParams(
            collective_id=0, has_side_effects=True, vmem_limit_bytes=67043328),
    )(tokens, d_out, jnp.asarray(cosine), jnp.asarray(sine), w_query, w_down.T, w_up,
      latent_gain.reshape(1, 64))
    return finish(fin, clip, token_grad)


def solution(mesh):
    split = Mesh(mesh.devices.reshape(4, 4, 4, 2), NODE_LOCAL)
    return jax.shard_map(
        per_device,
        mesh=split,
        in_specs=(
            P(NODE_LOCAL, None),
            P(NODE_LOCAL, None),
            P(LOCAL, None),
            P(LOCAL, None),
            P(LOCAL, None),
            P(LOCAL),
        ),
        out_specs=(
            P(NODE_LOCAL, None),
            P(NODE_LOCAL, None),
            P(NODE_LOCAL, None),
            P(NODE_LOCAL),
            P(NODE_LOCAL, None),
        ),
        check_vma=False,
    )
```

time: 127 us -> 108 us (0.85)
  local copies, waits for them, and re-layouts: 11.6 us -> 0 us
  other arithmetic: 3.95 us -> 0 us
  Pallas kernels: 110 us -> 107 us
    pallas_call x1, Pallas kernels: 110 us -> 103 us  [per_device(): pl.pallas_call(mega, out_shape=(jax.ShapeDtypeStruct((2, 32, GTOT), F32),...]
    unnamed x3 -> x0, local copies, waits for them, and re-layouts: 5.03 us -> none
    pallas_call x0 -> x1, Pallas kernels: none -> 4.07 us  [finish(): pl.pallas_call(last_step, out_shape=(jax.ShapeDtypeStruct((16, 1536), F32...]
    mul x4 -> x0, other arithmetic: 3.94 us -> none  [the longest x1 1.34 us: per_device(): grad_down * clip]
    squeeze x3 -> x0, local copies, waits for them, and re-layouts: 2.25 us -> none  [the longest x1 0.8 us: per_device(): rows[0, :, :384]]
    slice x2 -> x0, local copies, waits for them, and re-layouts: 2.02 us -> none  [the longest x1 1.19 us: per_device(): clip = clip[0, 0]]
    mul x3 -> x0, local copies, waits for them, and re-layouts: 1.41 us -> none  [the longest x1 0.74 us: per_device(): grad_query * clip]
where the time goes in v2:
time: 108 us
  Pallas kernels  107 us (99%)
    pallas_call x1, Pallas kernels, per_device(): pl.pallas_call(mega, out_shape=(jax.ShapeDtypeStruct((2, 32, GTOT), F32),...  103 us
    pallas_call x1, Pallas kernels, finish(): pl.pallas_call(last_step, out_shape=(jax.ShapeDtypeStruct((16, 1536), F32...  4.07 us

profile of v2, /device:TPU:1, one launch (start us, length us, event | category | flops | bytes accessed | tf_op | source)
XLA Modules:
  0.0 108.0 jit_solution(4706074723275871085)
XLA Ops:
  0.6 103.1 %shard_map.119 = (f32[2,32,1408]{2,1,0:T(8,128)}, f32[8,128]{1,0:T(8,128)}, bf16[512,2048]{1,0:T(8,128)(2,1)}) custom-call(bf16[512,2048]{1,0:T(8,128)(2,1)} %tokens_hbm.1, bf16[512,1024]{1,0:T(8,128)(2,1)} %dout_hbm.1, f32[512,128]{1,0:T(8,128)} %constant.4.clone.cos_hbm, f32[512,128]{1,0:T(8,128)} %constant.5.clone.sin_hbm, bf16[256,1536]{1,0:T(8,128)(2,1)} %wq_ref.1, ...), custom_call_target="tpu_custom_call" | custom-call | tf_op jit(solution)/shard_map/pallas_call | solution.py:719
  103.8 4.1 %shard_map.120 = (f32[16,1536]{1,0:T(8,128)}, f32[16,576]{1,0:T(8,128)}, f32[4,2048]{1,0:T(4,128)}, f32[4]{0:T(128)}, bf16[512,2048]{1,0:T(8,128)(2,1)}) custom-call(f32[2,32,1408]{2,1,0:T(8,128)} %get-tuple-element.8.fin_ref, f32[8,128]{1,0:T(8,128)} %get-tuple-element.9.clip_ref, bf16[512,2048]{1,0:T(8,128)(2,1)} %get-tuple-element.10.tg_in), custom_call_target="tpu_custom_call" | custom-call | tf_op jit(solution)/shard_map/pallas_call | solution.py:699

commit v3 on v2

v3 whole, which is shorter than its diff:
```python
import math

import jax
import jax.numpy as jnp
import numpy as np
from jax import lax
from jax.experimental import pallas as pl
from jax.experimental.pallas import tpu as pltpu
from jax.sharding import Mesh
from jax.sharding import PartitionSpec as P

H = 8
DN = 128
DR = 64
DV = 128
KVL = 512
SEQ = 512
D = 2048
NPARAM = 5374464
EPSILON = 1e-06
ROPE_BASE = 10000.0
LOCAL = ("local_0", "local_1")
NODE_LOCAL = ("node_0", "node_1", "local_0", "local_1")
MESH = pl.DeviceIdType.MESH
AZ, AX, AY, AC = NODE_LOCAL

WCOL = 2176
SUBS = ((0, 640), (640, 1408), (1408, 2176))
SCALE = 1.0 / math.sqrt(DN + DR)
AXES = ((AZ, AX, AY), (AX, AY, AZ), (AY, AZ, AX))
UNITS = tuple((w,) + AXES[n % 3] for n, w in enumerate((256, 256, 256, 256, 256, 128)))
GOFF = (0, 256, 512, 768, 1024, 1280)
GTOT = 1408
F32 = jnp.float32
BF16 = jnp.bfloat16


def rope_constants():
    position = np.arange(SEQ, dtype=np.float32)[:, None]
    freq = np.float32(ROPE_BASE) ** (-np.arange(DR // 2, dtype=np.float32) * np.float32(2.0 / DR))
    angle = (position * freq[None, :].astype(np.float32)).astype(np.float32)
    cosine = np.cos(angle).astype(np.float32)
    sine = np.sin(angle).astype(np.float32)
    return np.concatenate([cosine] * 4, 1), np.concatenate([-sine, sine] * 2, 1)


def nt(a, b):
    return lax.dot_general(a, b, (((1,), (1,)), ((), ())), preferred_element_type=F32)


def nn(a, b):
    return jnp.dot(a, b, preferred_element_type=F32)


def tn(a, b):
    return lax.dot_general(a, b, (((0,), (0,)), ((), ())), preferred_element_type=F32)


def mega(
    tokens_hbm, dout_hbm, cos_hbm, sin_hbm, wq_hbm, wd_hbm, wu_hbm, gain_hbm,
    fin_ref, clip_ref, tg_hbm,
    tokens, dout, cosr, sinr, wbuf, ubuf, gbuf, tokt, acc, qrope, qnope, nrm, nrt, ng, krp, dkr,
    jb, jp, kvg, kvgp, rg, rgp, rgf, invr, gmat, tgb, nbuf, wq_ref, wd_ref, gain_ref, lsem, ssem, rsem, *rest,
):
    nu = len(UNITS)
    part, own, rx, ra, part2, rx2, ra2, part3, ra3 = (rest[n * nu:(n + 1) * nu] for n in range(9))
    iz, ix, iy, ic = (lax.axis_index(a) for a in NODE_LOCAL)
    at = {AZ: iz, AX: ix, AY: iy}
    other = 1 - ic
    STEP = {(a, by): lax.rem(at[a] + (by + 4), 4) for a in at for by in (-1, 0, 1, 2)}

    def step(axis, by):
        return STEP[axis, by]

    recv_table, send_table, owed = {}, {}, []
    scope = []

    def mark(name):
        while scope:
            scope.pop().__exit__(None, None, None)
        if name:
            scope.append(jax.named_scope(name))
            scope[-1].__enter__()

    mark("start")

    def index(table, key):
        return table.setdefault(key, len(table))

    def send(key, src, dst, peer, outgoing=None):
        if outgoing is None:
            outgoing = key
            owed.append((key, src))
        pltpu.make_async_remote_copy(
            src_ref=src, dst_ref=dst,
            send_sem=ssem.at[index(send_table, outgoing)], recv_sem=rsem.at[index(recv_table, key)],
            device_id=peer, device_id_type=MESH).start()

    def arrived(key, ref):
        pltpu.make_async_remote_copy(
            src_ref=ref, dst_ref=ref, send_sem=ssem.at[0], recv_sem=rsem.at[index(recv_table, key)],
            device_id=mate, device_id_type=MESH).wait_recv()

    def left(key, ref):
        pltpu.make_async_remote_copy(
            src_ref=ref, dst_ref=ref, send_sem=ssem.at[index(send_table, key)], recv_sem=rsem.at[0],
            device_id=mate, device_id_type=MESH).wait_send()

    mate = {AC: other}
    barrier = pltpu.get_barrier_semaphore()
    for axis in (AZ, AX, AY):
        for by in (1, -1, 2):
            pl.semaphore_signal(barrier, inc=1, device_id={axis: step(axis, by)}, device_id_type=MESH)
    pl.semaphore_signal(barrier, inc=1, device_id=mate, device_id_type=MESH)

    loads = {}

    def load(name, src, dst):
        d = pltpu.make_async_copy(src, dst, lsem.at[len(loads)])
        d.start()
        loads[name] = d

    for p in range(8):
        pltpu.make_async_copy(wu_hbm.at[:, p * 256:(p + 1) * 256], ubuf.at[iy, ic, p], lsem.at[8]).start()

    load("down", wd_hbm, wd_ref)
    load("query", wq_hbm, wq_ref)
    load("gain", gain_hbm, gain_ref)
    load("tokens", tokens_hbm, tokens)
    load("dout", dout_hbm, dout)
    load("cos", cos_hbm, cosr)
    load("sin", sin_hbm, sinr)

    loads["down"].wait()
    down = jnp.concatenate([wd_ref[...], jnp.zeros((64, 256), BF16)], 0)
    wbuf[iy, ic, :, :, 0:640] = down.T.reshape(8, 32, 640)
    loads["query"].wait()
    for n in range(4):
        lo = 640 + n * 384
        h = n * 384
        both = jnp.concatenate([
            wq_ref[:, h:h + 128], wq_ref[:, h + 192:h + 320],
            wq_ref[:, h + 128:h + 192], wq_ref[:, h + 320:h + 384]], 1)
        wbuf[iy, ic, :, :, lo:lo + 384] = both.reshape(8, 32, 384)
    loads["gain"].wait()
    gbuf[iy, ic] = jnp.broadcast_to(
        jnp.concatenate([gain_ref[...].astype(F32), jnp.zeros((1, 64), F32)], 1), (8, 128))
    own_up = ubuf.at[iy, ic]
    pltpu.make_async_copy(own_up, own_up, lsem.at[8]).wait()
    pl.semaphore_wait(barrier, 10)

    RING = (AX, AZ)
    YO = (step(AY, -1), step(AY, 1), step(AY, 2))
    PIECE = {(k, by): k * 4 + step(RING[k], by) for k in range(2) for by in (-1, 0, 1, 2)}
    KINDS = (0, "u", 1, 2)

    def block_of(kind, yy, core):
        if kind == "u":
            return ubuf.at[yy, core]
        lo, hi = SUBS[kind]
        return wbuf.at[yy, core, :, :, lo:hi]

    def piece(kind, yy, k, by):
        if kind == "u":
            return ubuf.at[yy, ic, PIECE[k, by]]
        lo, hi = SUBS[kind]
        return wbuf.at[yy, ic, PIECE[k, by], :, lo:hi]

    def half_piece(kind, yy, k, by, d):
        if kind == "u":
            return ubuf.at[yy, ic, PIECE[k, by], d * 32:d * 32 + 32]
        lo, hi = SUBS[kind]
        return wbuf.at[yy, ic, PIECE[k, by], d * 16:d * 16 + 16, lo:hi]

    def span(kind, n):
        if kind == "u":
            return ubuf.at[0, 0, 0:n]
        lo, hi = SUBS[kind]
        return wbuf.at[0, 0, 0:n, :, lo:hi]

    def link_send(key, kind, r, axis, by):
        send(key, r, r, {axis: step(axis, by)}, ("links", kind))

    def piece_to_mate(kind, yo, k, by):
        r = piece(kind, YO[yo], k, by)
        send(("d", kind), r, r, mate, ("d", kind))

    def y_send(kind):
        for k in range(2):
            r = piece(kind, iy, k, 0)
            link_send(("y", kind), kind, r, AY, 1)
            link_send(("y", kind), kind, r, AY, -1)

    def pset(yo):
        return yo // 2

    def p_send(kind, k, yo):
        r = piece(kind, YO[yo], k, 0)
        link_send(("p", kind, pset(yo)), kind, r, RING[k], 1)
        link_send(("p", kind, pset(yo)), kind, r, RING[k], -1)

    def y_take(kind):
        arrived(("y", kind), span(kind, 4))
        for k in range(2):
            for d in range(2):
                half = half_piece(kind, YO[d], k, 0, d)
                link_send(("y2", kind), kind, half, AY, 1 if d == 0 else -1)
                p_send(kind, k, d)
        for k in range(2):
            for d in range(2):
                piece_to_mate(kind, d, k, 0)

    def y2_take(kind):
        arrived(("y2", kind), span(kind, 2))
        for k in range(2):
            p_send(kind, k, 2)
            piece_to_mate(kind, 2, k, 0)

    def p_take(kind, *yos):
        arrived(("p", kind, pset(yos[0])), span(kind, 4 * len(yos)))
        for yo in yos:
            for k in range(2):
                for d in range(2):
                    by = -1 if d == 0 else 1
                    half = half_piece(kind, YO[yo], k, by, d)
                    link_send(("p2", kind, pset(yo)), kind, half, RING[k], -by)
        for yo in yos:
            for k in range(2):
                for by in (-1, 1):
                    piece_to_mate(kind, yo, k, by)

    def p2_take(kind, *yos):
        arrived(("p2", kind, pset(yos[0])), span(kind, 2 * len(yos)))
        for yo in yos:
            for k in range(2):
                piece_to_mate(kind, yo, k, 2)

    def own_to_mate(kind):
        r = block_of(kind, iy, ic)
        send(("d", kind), r, r, mate, ("d", kind))

    def from_mate(kind):
        if kind == "u":
            arrived(("d", kind), ubuf.at[:, other])
        else:
            lo, hi = SUBS[kind]
            arrived(("d", kind), wbuf.at[:, other, :, :, lo:hi])

    def project(lo, hi):
        return nn(tokens[...], wbuf[:, :, :, :, lo:hi].reshape(2048, hi - lo))

    mark("gather")
    y_send(0)
    y_send("u")
    y_send(1)
    own_to_mate(0)
    g = gbuf.at[iy, ic]
    for n, by in enumerate((1, -1, 2)):
        send("g", g, g, {AY: step(AY, by)}, "g")
    send("gd", g, g, mate, "gd")
    own_to_mate("u")
    mark("y0")
    y_take(0)
    own_to_mate(1)
    mark("yu")
    y_take("u")
    y_send(2)
    own_to_mate(2)
    loads["tokens"].wait()
    mark("transpose")
    for z in range(2):
        tokt[z, :, :, :, 0:512] = tokens[:, z * 512:(z + 1) * 512].T.reshape(4, 4, 32, 512)
    mark("y20")
    y2_take(0)
    mark("p0a")
    p_take(0, 0, 1)
    mark("y1")
    y_take(1)
    mark("y2u")
    y2_take("u")
    mark("pua")
    p_take("u", 0, 1)
    mark("p0b")
    p_take(0, 2)
    mark("transpose")
    for z in range(2, 4):
        tokt[z, :, :, :, 0:512] = tokens[:, z * 512:(z + 1) * 512].T.reshape(4, 4, 32, 512)
    mark("y21")
    y2_take(1)
    mark("p1a")
    p_take(1, 0, 1)
    mark("pub")
    p_take("u", 2)
    mark("p20")
    p2_take(0, 0, 1)
    mark("y2")
    y_take(2)
    mark("p202")
    p2_take(0, 2)
    mark("p1b")
    p_take(1, 2)
    mark("y22")
    y2_take(2)
    mark("g")
    arrived("g", gbuf.at[0:3, 0])
    for by in (-1, 1, 2):
        gg = gbuf.at[step(AY, by), ic]
        send("gd", gg, gg, mate, "gd")
    mark("down")
    from_mate(0)
    acc[...] = project(*SUBS[0])
    mark("p2u")
    p2_take("u", 0, 1)
    p2_take("u", 2)
    mark("p2a")
    p_take(2, 0, 1)
    mark("p21")
    p2_take(1, 0, 1)
    p2_take(1, 2)
    mark("pre")
    arrived("gd", gbuf.at[:, other])

    for name in ("dout", "cos", "sin"):
        loads[name].wait()

    lane = lax.broadcasted_iota(jnp.int32, (1, 128), 1)
    low = lax.rem(lane, 64) < 32

    def swap(v):
        return jnp.where(low, pltpu.roll(v, 96, 1), pltpu.roll(v, 32, 1))

    def rot(v, sign):
        return v * cosr[...] + swap(v) * (sinr[...] * sign)

    gain = jnp.concatenate([gbuf[y, c, 0:1, 0:64] for y in range(4) for c in range(2)], 1)
    kr = rot(acc[:, 512:640], 1.0)
    krp[0] = jnp.where(lane < 64, kr, 0.0).astype(BF16)
    krp[1] = jnp.where(lane < 64, 0.0, pltpu.roll(kr, 64, 1)).astype(BF16)
    for n in range(4):
        rows = slice(n * 128, (n + 1) * 128)
        latent = acc[rows, 0:512]
        inv = lax.rsqrt(jnp.mean(latent * latent, axis=-1, keepdims=True) + EPSILON)
        unit = latent * inv
        acc[rows, 0:512] = unit
        invr[rows] = jnp.broadcast_to(inv, (128, 128))
        nrm[rows] = (unit * gain).astype(BF16)
    nrt[:, 0:512] = nrm[...].T
    send(("nrt",), nrt.at[:, 0:512], nrt.at[:, 512:1024], mate)
    ng[...] = jnp.zeros((512, 512), F32)
    dkr[...] = jnp.zeros((512, 128), F32)
    send(("tok",), tokt.at[:, :, :, :, 0:512], tokt.at[:, :, :, :, 512:1024], mate)
    mark("p2b")
    p_take(2, 2)
    mark("mateu")
    from_mate("u")
    mark("heads")

    tri = (lax.broadcasted_iota(jnp.int32, (256, 256), 0)
           <= lax.broadcasted_iota(jnp.int32, (256, 256), 1))

    def block(kf, v, qf, do):
        rows = kf.shape[0]
        s = nt(kf, qf) * SCALE
        masked = jnp.where(tri, s[rows - 256:], -1e30)
        s = masked if rows == 256 else jnp.concatenate([s[:rows - 256], masked], 0)
        w = jnp.exp(s - jnp.max(s, axis=0, keepdims=True))
        probs = w * (1.0 / jnp.sum(w, axis=0, keepdims=True))
        dp = nt(v, do)
        delta = jnp.sum(probs * dp, axis=0, keepdims=True)
        ds = (probs * (dp - delta) * SCALE).astype(BF16)
        return probs.astype(BF16), ds

    def queries(s):
        from_mate(s + 1)
        lo = SUBS[s + 1][0]
        q = project(lo, lo + 768)
        for m in range(2):
            n = 2 * s + m
            qnope[:, n * 256:(n + 1) * 256] = q[:, m * 384:m * 384 + 256].astype(BF16)
            rope = q[:, m * 384 + 256:m * 384 + 384].astype(BF16).astype(F32)
            qrope[:, n * 128:(n + 1) * 128] = rot(rope, 1.0).astype(BF16)

    def pair(n, carry):
        @pl.when(n == 0)
        def _():
            queries(0)

        @pl.when(n == 1)
        def _():
            p2_take(2, 0, 1)
            p2_take(2, 2)

        @pl.when(n == 2)
        def _():
            queries(1)

        half, m = n // 2, lax.rem(n, 2)
        qr = qrope[:, pl.ds(pl.multiple_of(n * 128, 128), 128)]
        total = None
        for e in range(2):
            h = 2 * n + e
            hc = pl.ds(pl.multiple_of(h * 128, 128), 128)
            jc = pl.ds(pl.multiple_of((m * 2 + e) * 128, 128), 128)
            u = ubuf[:, :, h].reshape(512, 256)
            kv = nn(nrm[...], u).astype(BF16)
            kf = jnp.concatenate([kv[:, :128], krp[e]], 1)
            v = kv[:, 128:]
            qf = jnp.concatenate([qnope[:, hc], qr], 1)
            do = dout[:, hc]
            pa, da = block(kf[:256], v[:256], qf[:256], do[:256])
            pb, db = block(kf, v, qf[256:], do[256:])
            dv = nn(pb, do[256:])
            dv = jnp.concatenate([dv[:256] + nn(pa, do[:256]), dv[256:]], 0)
            dk = nn(db, qf[256:])
            dk = jnp.concatenate([dk[:256] + nn(da, qf[:256]), dk[256:]], 0)
            dq = jnp.concatenate([tn(da, kf[:256]), tn(db, kf)], 0)
            jb[half, :, jc] = dq[:, :128].astype(BF16)
            total = dq[:, 128:] if e == 0 else total + dq[:, 128:]
            keep = lane < 64 if e == 0 else lane >= 64
            dkr[...] += jnp.where(keep, dk[:, 128:], 0.0)
            kg = dk[:, :128].astype(BF16)
            vg = dv.astype(BF16)
            kvg[half, 0, :, jc] = kg
            kvg[half, 1, :, jc] = vg
            ng[...] += nt(jnp.concatenate([kg, vg], 1), u)
        jb[half, :, pl.ds(pl.multiple_of(512 + m * 128, 128), 128)] = rot(total, -1.0).astype(BF16)
        return carry

    lax.fori_loop(0, 4, pair, 0)
    mark("post")
    send(("j",), jb.at[other, :, 0:768], jp.at[:, 0:768], mate)

    gterm = jnp.zeros((1, 512), F32)
    for n in range(4):
        rows = slice(n * 128, (n + 1) * 128)
        unit = acc[rows, 0:512]
        grad = ng[rows]
        gterm = gterm + jnp.sum(grad * unit, axis=0, keepdims=True)
        scaled = grad * gain
        inner = jnp.mean(scaled * unit, axis=-1, keepdims=True)
        value = (invr[rows, 0:1] * (scaled - unit * inner)).astype(BF16)
        jb[0, rows, 768:1024] = value[:, :256]
        jb[1, rows, 768:1024] = value[:, 256:]
    dk = dkr[...]
    rope = jnp.where(lane < 64, rot(dk + pltpu.roll(dk, 64, 1), -1.0), 0.0)
    rgf[...] = rope.astype(BF16)
    rg[0] = jnp.where(lane < 32, rope, 0.0).astype(BF16)
    rg[1] = jnp.where(lane < 32, pltpu.roll(rope, 96, 1), 0.0).astype(BF16)
    send(("kvg",), kvg.at[other], kvgp, mate)
    send(("jl",), jb.at[other, :, 768:1024], jp.at[:, 768:1024], mate)
    send(("rg",), rg.at[other], rgp, mate)
    column = jnp.broadcast_to(gterm, (128, 512)).T
    column = jnp.where(lane == 32, column, 0.0).reshape(64, 8, 128)
    gmat[...] = jnp.concatenate([column, jnp.zeros((64, 24, 128), F32)], 1).reshape(4, 4, 4, 32, 128)

    tgd = []

    def token_block():
        n = len(tgd)
        w = wbuf[n].reshape(512, WCOL)
        cols = [jb[0, :, 768:], jb[1, :, 768:], rgf[...]]
        for m in range(4):
            cols += [jb[m // 2, :, m % 2 * 256:m % 2 * 256 + 256],
                     jb[m // 2, :, 512 + m % 2 * 128:640 + m % 2 * 128]]
        tgb[n] = nt(jnp.concatenate(cols, 1), w).astype(BF16)
        d = pltpu.make_async_copy(tgb.at[n], tg_hbm.at[:, n * 512:(n + 1) * 512], lsem.at[9])
        d.start()
        tgd.append(d)

    mark("waitmate")
    arrived(("tok",), tokt.at[:, :, :, :, 512:1024])
    arrived(("nrt",), nrt.at[:, 512:1024])
    arrived(("j",), jp.at[:, 0:768])

    A, B = (0, 1, 2), (3, 4, 5)
    def keep(u, z, cols, value):
        g = u % 3
        value = value.astype(BF16)
        if g == 0:
            part[u][z, :, :, :, cols] = value
        elif g == 1:
            part[u][:, z, :, :, cols] = value
        else:
            for x in range(4):
                part[u][:, z, x, :, cols] = value[x]

    def token_rows(z):
        return tokt[z].reshape(512, 1024)

    def products_a():
        right = jnp.concatenate([jb[ic, :, 0:768], jp[:, 0:768]], 0)
        for z in range(4):
            both = nn(token_rows(z), right).reshape(4, 4, 32, 768)
            for u in A:
                keep(u, z, slice(0, 256), both[..., u * 256:u * 256 + 256])

    def products_b():
        right = jnp.concatenate([
            jnp.concatenate([jb[ic, :, 768:1024], rg[ic]], 1),
            jnp.concatenate([jp[:, 768:1024], rgp[...]], 1)], 0)
        for z in range(4):
            both = nn(token_rows(z), right).reshape(4, 4, 32, 384)
            for u in (3, 4):
                keep(u, z, slice(0, 128), both[..., (u - 3) * 128:(u - 2) * 128])
            keep(5, z, slice(0, 128), both[..., 256:] + gmat[z])
        for u in (3, 4):
            up = nn(nrt[...], jnp.concatenate([kvg[ic, u - 3], kvgp[u - 3]], 0))
            up = up.reshape(64, 8, 512)
            up = jnp.concatenate([up[:, :, j * 128:(j + 1) * 128] for j in range(4)], 1)
            up = up.reshape(4, 4, 4, 32, 128)
            for z in range(4):
                keep(u, z, slice(128, 256), up[z])

    def ways(axis):
        return {axis: step(axis, 1)}, {axis: step(axis, -1)}

    def ring_sends(phase, u, p, r, a):
        axis = UNITS[u][phase]
        right, left_ = ways(axis)
        far, near, back = (p[u].at[step(axis, by)] for by in (2, 1, -1))
        send(("x", phase, u), far.at[0:2], r[u].at[0], right, ("s", phase, u))
        send(("x", phase, u), far.at[2:4], r[u].at[1], left_, ("s", phase, u))
        send(("a", phase, u), near.at[2:4], a[u].at[0, 2:4], right, ("s", phase, u))
        send(("a", phase, u), back.at[0:2], a[u].at[1, 0:2], left_, ("s", phase, u))

    def relay(phase, us, p, r, a):
        for u in us:
            axis = UNITS[u][phase]
            right, left_ = ways(axis)
            near, back = (p[u].at[step(axis, by)] for by in (1, -1))
            arrived(("x", phase, u), r[u])
            near[0:2] = (near[0:2].astype(F32) + r[u][0].astype(F32)).astype(BF16)
            back[2:4] = (back[2:4].astype(F32) + r[u][1].astype(F32)).astype(BF16)
            send(("a", phase, u), near.at[0:2], a[u].at[0, 0:2], right, ("s", phase, u))
            send(("a", phase, u), back.at[2:4], a[u].at[1, 2:4], left_, ("s", phase, u))

    def second(u, t):
        return own[u].at[:, t] if u % 3 == 1 else own[u].at[t]

    def second_sends(us):
        for u in us:
            arrived(("a", 1, u), ra[u])
            total = part[u][at[UNITS[u][1]]].astype(F32) + (ra[u][0].astype(F32) + ra[u][1].astype(F32))
            own[u][...] = total
            if u % 3 == 1:
                for z in range(4):
                    part2[u][:, z] = total[z].astype(BF16)
            else:
                part2[u][...] = total.astype(BF16)
            ring_sends(2, u, part2, rx2, ra2)

    def third_sends(us):
        for u in us:
            arrived(("a", 2, u), ra2[u])
            mine = second(u, at[UNITS[u][2]])
            mine[...] += ra2[u][0].astype(F32) + ra2[u][1].astype(F32)
            for slot, by in enumerate((2, 1, -1)):
                part3[u][slot] = mine[step(UNITS[u][3], by)].astype(BF16)
                send(("a", 3, u), part3[u].at[slot], ra3[u].at[slot],
                     {UNITS[u][3]: step(UNITS[u][3], by)}, ("s", 3, u))

    def last_sums(us):
        for u in us:
            arrived(("a", 3, u), ra3[u])
            mine = second(u, at[UNITS[u][2]])[at[UNITS[u][3]]]
            fin_ref[ic, :, GOFF[u]:GOFF[u] + UNITS[u][0]] = mine + (
                ra3[u][0].astype(F32) + ra3[u][1].astype(F32) + ra3[u][2].astype(F32))

    mark("firstA")
    products_a()
    for u in A:
        ring_sends(1, u, part, rx, ra)
    mark("mateB")
    arrived(("kvg",), kvgp)
    arrived(("jl",), jp.at[:, 768:1024])
    arrived(("rg",), rgp)
    mark("productsB")
    products_b()
    for u in B:
        ring_sends(1, u, part, rx, ra)
    mark("tg")
    token_block()
    mark("relayA")
    relay(1, A, part, rx, ra)
    mark("tg")
    token_block()
    token_block()
    mark("relayB")
    relay(1, B, part, rx, ra)
    mark("tg")
    token_block()
    mark("secondA")
    second_sends(A)
    mark("secondB")
    second_sends(B)
    mark("relay2A")
    relay(2, A, part2, rx2, ra2)
    mark("relay2B")
    relay(2, B, part2, rx2, ra2)
    mark("thirdA")
    third_sends(A)
    mark("thirdB")
    third_sends(B)
    mark("lastA")
    last_sums(A)
    send(("fin", 0), fin_ref.at[ic, :, 0:768], fin_ref.at[ic, :, 0:768], mate)
    mark("lastB")
    last_sums(B)
    send(("fin", 1), fin_ref.at[ic, :, 768:GTOT], fin_ref.at[ic, :, 768:GTOT], mate)
    mark("fin")
    arrived(("fin", 0), fin_ref.at[other, :, 0:768])
    arrived(("fin", 1), fin_ref.at[other, :, 768:GTOT])

    both = fin_ref[...]
    tail = GTOT - 128
    gains = both[0, :, tail:] + both[1, :, tail:]
    body = both[:, :, :tail]
    squares = jnp.sum(jnp.sum(body * body, axis=0), axis=0, keepdims=True)
    row = sum(squares[:, n * 128:(n + 1) * 128] for n in range(10))
    ropes = jnp.where(lane == 32, 0.0, both[0, :, tail:] ** 2 + both[1, :, tail:] ** 2)
    ropes = ropes + jnp.where(lane == 32, gains * gains, 0.0)
    row = row + jnp.sum(ropes, axis=0, keepdims=True)
    row = jnp.broadcast_to(row, (8, 128))
    mark("norm")
    lead = ic == 1
    for n, axis in enumerate((AY, AX, AZ)):
        @pl.when(lead)
        def _():
            nbuf[n, 3] = row if n == 0 else (nbuf[n - 1, 0] + nbuf[n - 1, 1]) + (nbuf[n - 1, 2] + nbuf[n - 1, 3])
            for m, by in enumerate((1, -1, 2)):
                send(("n", n), nbuf.at[n, 3], nbuf.at[n, m], {axis: step(axis, by)}, ("n", n))

        @pl.when(lead)
        def _():
            arrived(("n", n), nbuf.at[n, 0:3])

    @pl.when(lead)
    def _():
        nbuf[3, 0] = (nbuf[2, 0] + nbuf[2, 1]) + (nbuf[2, 2] + nbuf[2, 3])
        send("nd", nbuf.at[3, 0], nbuf.at[3, 0], mate, "nd")
        for n in range(3):
            left(("n", n), nbuf.at[n, 0:3])
        left("nd", nbuf.at[3, 0])

    @pl.when(jnp.logical_not(lead))
    def _():
        arrived("nd", nbuf.at[3, 0])

    total = jnp.sum(nbuf[3, 0], axis=-1, keepdims=True)
    clip = jnp.minimum(1.0, lax.rsqrt(total / NPARAM + 1e-06))
    clip_ref[...] = jnp.broadcast_to(clip, (8, 128))

    mark("drain")
    for key, ref in owed:
        left(key, ref)
    left("g", gbuf.at[0:3, 0])
    left("gd", gbuf.at[:, 0])
    for kind in KINDS:
        if kind == "u":
            left(("links", kind), ubuf.at[0:3, 0])
            left(("d", kind), ubuf.at[:, 0])
        else:
            lo, hi = SUBS[kind]
            left(("links", kind), wbuf.at[0:3, 0, :, :, lo:hi])
            left(("d", kind), wbuf.at[:, 0, :, :, lo:hi])
    for u in range(nu):
        left(("s", 1, u), part[u].at[0:3])
        left(("s", 2, u), part2[u].at[0:3])
        left(("s", 3, u), part3[u])
    pltpu.make_async_copy(tgb, tgb, lsem.at[9]).wait()
    mark(None)
    assert len(recv_table) == NRECV and len(send_table) == NSEND, (len(recv_table), len(send_table))


NRECV = 72
NSEND = 40


def scratch():
    v = pltpu.VMEM
    dma = pltpu.SemaphoreType.DMA
    shapes = [
        v((512, 2048), BF16), v((512, 1024), BF16), v((512, 128), F32), v((512, 128), F32),
        v((4, 2, 8, 32, WCOL), BF16), v((4, 2, 8, 64, 256), BF16), v((4, 2, 8, 128), F32),
        v((4, 4, 4, 32, 1024), BF16), v((512, 640), F32),
        v((512, 512), BF16), v((512, 1024), BF16), v((512, 512), BF16), v((512, 1024), BF16),
        v((512, 512), F32), v((2, 512, 128), BF16), v((512, 128), F32),
        v((2, 512, 1024), BF16), v((512, 1024), BF16), v((2, 2, 512, 512), BF16), v((2, 512, 512), BF16),
        v((2, 512, 128), BF16), v((512, 128), BF16), v((512, 128), BF16), v((512, 128), F32),
        v((4, 4, 4, 32, 128), F32), v((4, 512, 512), BF16), v((4, 4, 8, 128), F32),
        v((256, 1536), BF16), v((576, 256), BF16), v((1, 64), BF16),
        dma((10,)), dma((NSEND,)), dma((NRECV,)),
    ]
    ws = [w for w, *_ in UNITS]
    shapes += [v((4, 4, 4, 32, w), BF16) for w in ws]
    shapes += [v((4, 4, 32, w), F32) for w in ws]
    shapes += [v((2, 2, 4, 32, w), BF16) for w in ws]
    shapes += [v((2, 4, 4, 32, w), BF16) for w in ws]
    shapes += [v((4, 4, 32, w), BF16) for w in ws]
    shapes += [v((2, 2, 32, w), BF16) for w in ws]
    shapes += [v((2, 4, 32, w), BF16) for w in ws]
    shapes += [v((3, 32, w), BF16) for w in ws]
    shapes += [v((3, 32, w), BF16) for w in ws]
    return shapes


def last_step(fin_hbm, clip_hbm, tg_in, gq_ref, gd_ref, gu_ref, gg_ref, tg_out,
              fin_ref, clip_ref, stage, isem, osem):
    ic = lax.axis_index(AC)
    first_reads = []
    for n, (src, dst) in enumerate(((fin_hbm, fin_ref), (clip_hbm, clip_ref))):
        d = pltpu.make_async_copy(src, dst, isem.at[4 + n])
        d.start()
        first_reads.append(d)
    reads = []
    for n in range(4):
        rows = slice(n * 128, (n + 1) * 128)
        d = pltpu.make_async_copy(tg_in.at[rows], stage.at[n], isem.at[n])
        d.start()
        reads.append(d)
    writes = []
    for n in range(4):
        rows_n = slice(n * 128, (n + 1) * 128)
        reads[n].wait()
        d = pltpu.make_async_copy(stage.at[n], tg_out.at[rows_n], osem.at[n])
        d.start()
        writes.append(d)
    for d in first_reads:
        d.wait()
    clip = clip_ref[0:1, 0:1]
    first = ic == 0

    def rows(half, cols):
        return jnp.where(first, fin_ref[half, 0:16, cols], fin_ref[half, 16:32, cols]) * clip

    def cols(lo):
        return slice(lo, lo + 128)

    for n in range(4):
        half, m = n // 2, n % 2
        rope = rows(half, cols(512 + m * 128))
        gq_ref[:, n * 384:(n + 1) * 384] = jnp.concatenate(
            [rows(half, cols(m * 256)), rope[:, :64], rows(half, cols(m * 256 + 128)), rope[:, 64:]], 1)
        gd_ref[:, n * 128:(n + 1) * 128] = rows(half, cols(768 + m * 256))
    tail = slice(GTOT - 128, GTOT)
    gd_ref[:, 512:576] = jnp.concatenate([rows(0, tail)[:, :32], rows(1, tail)[:, :32]], 1)
    for h in range(H):
        half, j = h // 4, h % 4
        for u in range(2):
            block = fin_ref[half, j * 8:j * 8 + 8, cols(896 + u * 256)] * clip
            gu_ref[:, h * 256 + u * 128:h * 256 + u * 128 + 128] = jnp.where(first, block[0:4], block[4:8])
    gain = (fin_ref[0, 0:8, tail] + fin_ref[1, 0:8, tail]) * clip
    gain = jnp.where(first, gain[0:4], gain[4:8])
    spread = (lax.broadcasted_iota(jnp.int32, (4, 128), 0)
              == lax.broadcasted_iota(jnp.int32, (4, 128), 1))
    gg_ref[...] = jnp.sum(jnp.where(spread, gain[:, 32:33], 0.0), axis=0)[0:4]
    for d in writes:
        d.wait()


def finish(fin, clip, token_grad):
    vm = pl.BlockSpec(memory_space=pltpu.VMEM)
    anyspace = pl.BlockSpec(memory_space=pl.ANY)
    return pl.pallas_call(
        last_step,
        out_shape=(
            jax.ShapeDtypeStruct((16, 1536), F32),
            jax.ShapeDtypeStruct((16, 576), F32),
            jax.ShapeDtypeStruct((4, 2048), F32),
            jax.ShapeDtypeStruct((4,), F32),
            jax.ShapeDtypeStruct((SEQ, D), BF16),
        ),
        in_specs=[anyspace] * 3,
        out_specs=(vm, vm, vm, vm, anyspace),
        scratch_shapes=[
            pltpu.VMEM((2, 32, GTOT), F32), pltpu.VMEM((8, 128), F32),
            pltpu.VMEM((4, 128, D), BF16), pltpu.SemaphoreType.DMA((6,)), pltpu.SemaphoreType.DMA((4,))],
    )(fin, clip, token_grad)


def per_device(tokens, d_out, w_query, w_down, w_up, latent_gain):
    cosine, sine = rope_constants()
    vm = pl.BlockSpec(memory_space=pltpu.VMEM)
    anyspace = pl.BlockSpec(memory_space=pl.ANY)
    fin, clip, token_grad = pl.pallas_call(
        mega,
        out_shape=(
            jax.ShapeDtypeStruct((2, 32, GTOT), F32),
            jax.ShapeDtypeStruct((8, 128), F32),
            jax.ShapeDtypeStruct((SEQ, D), BF16),
        ),
        in_specs=[anyspace] * 8,
        out_specs=(vm, vm, anyspace),
        scratch_shapes=scratch(),
        compiler_params=pltpu.CompilerParams(
            collective_id=0, has_side_effects=True, vmem_limit_bytes=67043328),
    )(tokens, d_out, jnp.asarray(cosine), jnp.asarray(sine), w_query, w_down.T, w_up,
      latent_gain.reshape(1, 64))
    return finish(fin, clip, token_grad)


def solution(mesh):
    split = Mesh(mesh.devices.reshape(4, 4, 4, 2), NODE_LOCAL)
    return jax.shard_map(
        per_device,
        mesh=split,
        in_specs=(
            P(NODE_LOCAL, None),
            P(NODE_LOCAL, None),
            P(LOCAL, None),
            P(LOCAL, None),
            P(LOCAL, None),
            P(LOCAL),
        ),
        out_specs=(
            P(NODE_LOCAL, None),
            P(NODE_LOCAL, None),
            P(NODE_LOCAL, None),
            P(NODE_LOCAL),
            P(NODE_LOCAL, None),
        ),
        check_vma=False,
    )
```

time: 108 us -> 101 us (0.935)
  Pallas kernels: 107 us -> 99.7 us
    pallas_call x1, Pallas kernels: 103 us -> 96.5 us  [per_device(): pl.pallas_call(mega, out_shape=(jax.ShapeDtypeStruct((2, 32, GTOT), F32),...]
where the time goes in v3:
time: 101 us
  Pallas kernels  99.7 us (99%)
    pallas_call x1, Pallas kernels, per_device(): pl.pallas_call(mega, out_shape=(jax.ShapeDtypeStruct((2, 32, GTOT), F32),...  96.5 us
    pallas_call x1, Pallas kernels, finish(): pl.pallas_call(last_step, out_shape=(jax.ShapeDtypeStruct((16, 1536), F32...  3.22 us

profile of v3, /device:TPU:1, one launch (start us, length us, event | category | flops | bytes accessed | tf_op | source)
XLA Modules:
  0.0 100.5 jit_solution(12386439399215206419)
XLA Ops:
  0.6 96.5 %shard_map.119 = (f32[2,32,1408]{2,1,0:T(8,128)}, f32[8,128]{1,0:T(8,128)}, bf16[512,2048]{1,0:T(8,128)(2,1)}) custom-call(bf16[512,2048]{1,0:T(8,128)(2,1)} %tokens_hbm.1, bf16[512,1024]{1,0:T(8,128)(2,1)} %dout_hbm.1, f32[512,128]{1,0:T(8,128)} %constant.4.clone.cos_hbm, f32[512,128]{1,0:T(8,128)} %constant.5.clone.sin_hbm, bf16[256,1536]{1,0:T(8,128)(2,1)} %wq_hbm.1, ...), custom_call_target="tpu_custom_call" | custom-call | tf_op jit(solution)/shard_map/pallas_call | solution.py:785
  97.1 3.2 %shard_map.120 = (f32[16,1536]{1,0:T(8,128)}, f32[16,576]{1,0:T(8,128)}, f32[4,2048]{1,0:T(4,128)}, f32[4]{0:T(128)}, bf16[512,2048]{1,0:T(8,128)(2,1)}) custom-call(f32[2,32,1408]{2,1,0:T(8,128)} %get-tuple-element.8.fin_hbm, f32[8,128]{1,0:T(8,128)} %get-tuple-element.9.clip_hbm, bf16[512,2048]{1,0:T(8,128)(2,1)} %get-tuple-element.10.tg_in), custom_call_target="tpu_custom_call" | custom-call | tf_op jit(solution)/shard_map/pallas_call | solution.py:764

commit v4 on v3

--- a/solution.py
+++ b/solution.py
@@ -28,8 +28,8 @@
 SUBS = ((0, 640), (640, 1408), (1408, 2176))
 SCALE = 1.0 / math.sqrt(DN + DR)
 AXES = ((AZ, AX, AY), (AX, AY, AZ), (AY, AZ, AX))
-UNITS = tuple((w,) + AXES[n % 3] for n, w in enumerate((256, 256, 256, 256, 256, 128)))
-GOFF = (0, 256, 512, 768, 1024, 1280)
+UNITS = tuple((w,) + AXES[n % 3] for n, w in enumerate((128,) * 6 + (256, 256, 128)))
+GOFF = (0, 128, 256, 384, 512, 640, 768, 1024, 1280)
 GTOT = 1408
 F32 = jnp.float32
 BF16 = jnp.bfloat16
@@ -348,7 +348,7 @@
     send(("nrt",), nrt.at[:, 0:512], nrt.at[:, 512:1024], mate)
     ng[...] = jnp.zeros((512, 512), F32)
     dkr[...] = jnp.zeros((512, 128), F32)
-    send(("tok",), tokt.at[:, :, :, :, 0:512], tokt.at[:, :, :, :, 512:1024], mate)
+    send("tok", tokt.at[:, :, :, :, 0:512], tokt.at[:, :, :, :, 512:1024], mate)
     mark("p2b")
     p_take(2, 2)
     mark("mateu")
@@ -370,6 +370,104 @@
         ds = (probs * (dp - delta) * SCALE).astype(BF16)
         return probs.astype(BF16), ds
 
+    A0, A1, B = (0, 1, 2), (3, 4, 5), (6, 7, 8)
+    def keep(u, z, cols, value):
+        g = u % 3
+        value = value.astype(BF16)
+        if g == 0:
+            part[u][z, :, :, :, cols] = value
+        elif g == 1:
+            part[u][:, z, :, :, cols] = value
+        else:
+            for x in range(4):
+                part[u][:, z, x, :, cols] = value[x]
+
+    def token_rows(z):
+        return tokt[z].reshape(512, 1024)
+
+    def products(slot):
+        cols = slice(slot * 384, slot * 384 + 384)
+        right = jnp.concatenate([jb[ic, :, cols], jp[:, cols]], 0)
+        us = A1 if slot else A0
+        for z in range(4):
+            both = nn(token_rows(z), right).reshape(4, 4, 32, 384)
+            for n, u in enumerate(us):
+                keep(u, z, slice(0, 128), both[..., n * 128:n * 128 + 128])
+        for u in us:
+            ring_sends(1, u, part, rx, ra)
+
+    def products_b():
+        right = jnp.concatenate([
+            jnp.concatenate([jb[ic, :, 768:1024], rg[ic]], 1),
+            jnp.concatenate([jp[:, 768:1024], rgp[...]], 1)], 0)
+        for z in range(4):
+            both = nn(token_rows(z), right).reshape(4, 4, 32, 384)
+            for u in (6, 7):
+                keep(u, z, slice(0, 128), both[..., (u - 6) * 128:(u - 5) * 128])
+            keep(8, z, slice(0, 128), both[..., 256:] + gmat[z])
+        for u in (6, 7):
+            up = nn(nrt[...], jnp.concatenate([kvg[ic, u - 6], kvgp[u - 6]], 0))
+            up = up.reshape(64, 8, 512)
+            up = jnp.concatenate([up[:, :, j * 128:(j + 1) * 128] for j in range(4)], 1)
+            up = up.reshape(4, 4, 4, 32, 128)
+            for z in range(4):
+                keep(u, z, slice(128, 256), up[z])
+
+    def ways(axis):
+        return {axis: step(axis, 1)}, {axis: step(axis, -1)}
+
+    def ring_sends(phase, u, p, r, a):
+        axis = UNITS[u][phase]
+        right, left_ = ways(axis)
+        far, near, back = (p[u].at[step(axis, by)] for by in (2, 1, -1))
+        send(("x", phase, u), far.at[0:2], r[u].at[0], right, ("s", phase, u))
+        send(("x", phase, u), far.at[2:4], r[u].at[1], left_, ("s", phase, u))
+        send(("a", phase, u), near.at[2:4], a[u].at[0, 2:4], right, ("s", phase, u))
+        send(("a", phase, u), back.at[0:2], a[u].at[1, 0:2], left_, ("s", phase, u))
+
+    def relay(phase, us, p, r, a):
+        for u in us:
+            axis = UNITS[u][phase]
+            right, left_ = ways(axis)
+            near, back = (p[u].at[step(axis, by)] for by in (1, -1))
+            arrived(("x", phase, u), r[u])
+            near[0:2] = (near[0:2].astype(F32) + r[u][0].astype(F32)).astype(BF16)
+            back[2:4] = (back[2:4].astype(F32) + r[u][1].astype(F32)).astype(BF16)
+            send(("a", phase, u), near.at[0:2], a[u].at[0, 0:2], right, ("s", phase, u))
+            send(("a", phase, u), back.at[2:4], a[u].at[1, 2:4], left_, ("s", phase, u))
+
+    def second(u, t):
+        return own[u].at[:, t] if u % 3 == 1 else own[u].at[t]
+
+    def second_sends(us):
+        for u in us:
+            arrived(("a", 1, u), ra[u])
+            total = part[u][at[UNITS[u][1]]].astype(F32) + (ra[u][0].astype(F32) + ra[u][1].astype(F32))
+            own[u][...] = total
+            if u % 3 == 1:
+                for z in range(4):
+                    part2[u][:, z] = total[z].astype(BF16)
+            else:
+                part2[u][...] = total.astype(BF16)
+            ring_sends(2, u, part2, rx2, ra2)
+
+    def third_sends(us):
+        for u in us:
+            arrived(("a", 2, u), ra2[u])
+            mine = second(u, at[UNITS[u][2]])
+            mine[...] += ra2[u][0].astype(F32) + ra2[u][1].astype(F32)
+            for slot, by in enumerate((2, 1, -1)):
+                part3[u][slot] = mine[step(UNITS[u][3], by)].astype(BF16)
+                send(("a", 3, u), part3[u].at[slot], ra3[u].at[slot],
+                     {UNITS[u][3]: step(UNITS[u][3], by)}, ("s", 3, u))
+
+    def last_sums(us):
+        for u in us:
+            arrived(("a", 3, u), ra3[u])
+            mine = second(u, at[UNITS[u][2]])[at[UNITS[u][3]]]
+            fin_ref[ic, :, GOFF[u]:GOFF[u] + UNITS[u][0]] = mine + (
+                ra3[u][0].astype(F32) + ra3[u][1].astype(F32) + ra3[u][2].astype(F32))
+
     def queries(s):
         from_mate(s + 1)
         lo = SUBS[s + 1][0]
@@ -393,42 +491,58 @@
         @pl.when(n == 2)
         def _():
             queries(1)
-
-        half, m = n // 2, lax.rem(n, 2)
+            arrived("tok", tokt.at[:, :, :, :, 512:1024])
+            arrived("j0", jp.at[:, 0:384])
+            products(0)
+
+        half, m = lax.rem(n, 2), n // 2
+        base = m * 384
         qr = qrope[:, pl.ds(pl.multiple_of(n * 128, 128), 128)]
-        total = None
+        stage = []
         for e in range(2):
             h = 2 * n + e
             hc = pl.ds(pl.multiple_of(h * 128, 128), 128)
-            jc = pl.ds(pl.multiple_of((m * 2 + e) * 128, 128), 128)
             u = ubuf[:, :, h].reshape(512, 256)
             kv = nn(nrm[...], u).astype(BF16)
             kf = jnp.concatenate([kv[:, :128], krp[e]], 1)
             v = kv[:, 128:]
             qf = jnp.concatenate([qnope[:, hc], qr], 1)
             do = dout[:, hc]
-            pa, da = block(kf[:256], v[:256], qf[:256], do[:256])
-            pb, db = block(kf, v, qf[256:], do[256:])
+            stage.append((u, kf, v, qf, do))
+        mids = []
+        for u, kf, v, qf, do in stage:
+            mids.append((block(kf[:256], v[:256], qf[:256], do[:256]), block(kf, v, qf[256:], do[256:])))
+        total = None
+        for e in range(2):
+            u, kf, v, qf, do = stage[e]
+            (pa, da), (pb, db) = mids[e]
             dv = nn(pb, do[256:])
             dv = jnp.concatenate([dv[:256] + nn(pa, do[:256]), dv[256:]], 0)
             dk = nn(db, qf[256:])
             dk = jnp.concatenate([dk[:256] + nn(da, qf[:256]), dk[256:]], 0)
             dq = jnp.concatenate([tn(da, kf[:256]), tn(db, kf)], 0)
-            jb[half, :, jc] = dq[:, :128].astype(BF16)
+            jb[half, :, pl.ds(pl.multiple_of(base + e * 128, 128), 128)] = dq[:, :128].astype(BF16)
             total = dq[:, 128:] if e == 0 else total + dq[:, 128:]
-            keep = lane < 64 if e == 0 else lane >= 64
-            dkr[...] += jnp.where(keep, dk[:, 128:], 0.0)
+            keep_lanes = lane < 64 if e == 0 else lane >= 64
+            dkr[...] += jnp.where(keep_lanes, dk[:, 128:], 0.0)
             kg = dk[:, :128].astype(BF16)
             vg = dv.astype(BF16)
+            jc = pl.ds(pl.multiple_of((m * 2 + e) * 128, 128), 128)
             kvg[half, 0, :, jc] = kg
             kvg[half, 1, :, jc] = vg
             ng[...] += nt(jnp.concatenate([kg, vg], 1), u)
-        jb[half, :, pl.ds(pl.multiple_of(512 + m * 128, 128), 128)] = rot(total, -1.0).astype(BF16)
+        jb[half, :, pl.ds(pl.multiple_of(base + 256, 128), 128)] = rot(total, -1.0).astype(BF16)
+
+        @pl.when(n == 1)
+        def _():
+            send("j0", jb.at[other, :, 0:384], jp.at[:, 0:384], mate, "j0")
+
         return carry
 
     lax.fori_loop(0, 4, pair, 0)
     mark("post")
-    send(("j",), jb.at[other, :, 0:768], jp.at[:, 0:768], mate)
+    send("j1", jb.at[other, :, 384:768], jp.at[:, 384:768], mate)
+    relay(1, A0, part, rx, ra)
 
     gterm = jnp.zeros((1, 512), F32)
     for n in range(4):
@@ -459,118 +573,19 @@
         n = len(tgd)
         w = wbuf[n].reshape(512, WCOL)
         cols = [jb[0, :, 768:], jb[1, :, 768:], rgf[...]]
-        for m in range(4):
-            cols += [jb[m // 2, :, m % 2 * 256:m % 2 * 256 + 256],
-                     jb[m // 2, :, 512 + m % 2 * 128:640 + m % 2 * 128]]
+        cols += [jb[m % 2, :, m // 2 * 384:m // 2 * 384 + 384] for m in range(4)]
         tgb[n] = nt(jnp.concatenate(cols, 1), w).astype(BF16)
         d = pltpu.make_async_copy(tgb.at[n], tg_hbm.at[:, n * 512:(n + 1) * 512], lsem.at[9])
         d.start()
         tgd.append(d)
 
     mark("waitmate")
-    arrived(("tok",), tokt.at[:, :, :, :, 512:1024])
     arrived(("nrt",), nrt.at[:, 512:1024])
-    arrived(("j",), jp.at[:, 0:768])
-
-    A, B = (0, 1, 2), (3, 4, 5)
-    def keep(u, z, cols, value):
-        g = u % 3
-        value = value.astype(BF16)
-        if g == 0:
-            part[u][z, :, :, :, cols] = value
-        elif g == 1:
-            part[u][:, z, :, :, cols] = value
-        else:
-            for x in range(4):
-                part[u][:, z, x, :, cols] = value[x]
-
-    def token_rows(z):
-        return tokt[z].reshape(512, 1024)
-
-    def products_a():
-        right = jnp.concatenate([jb[ic, :, 0:768], jp[:, 0:768]], 0)
-        for z in range(4):
-            both = nn(token_rows(z), right).reshape(4, 4, 32, 768)
-            for u in A:
-                keep(u, z, slice(0, 256), both[..., u * 256:u * 256 + 256])
-
-    def products_b():
-        right = jnp.concatenate([
-            jnp.concatenate([jb[ic, :, 768:1024], rg[ic]], 1),
-            jnp.concatenate([jp[:, 768:1024], rgp[...]], 1)], 0)
-        for z in range(4):
-            both = nn(token_rows(z), right).reshape(4, 4, 32, 384)
-            for u in (3, 4):
-                keep(u, z, slice(0, 128), both[..., (u - 3) * 128:(u - 2) * 128])
-            keep(5, z, slice(0, 128), both[..., 256:] + gmat[z])
-        for u in (3, 4):
-            up = nn(nrt[...], jnp.concatenate([kvg[ic, u - 3], kvgp[u - 3]], 0))
-            up = up.reshape(64, 8, 512)
-            up = jnp.concatenate([up[:, :, j * 128:(j + 1) * 128] for j in range(4)], 1)
-            up = up.reshape(4, 4, 4, 32, 128)
-            for z in range(4):
-                keep(u, z, slice(128, 256), up[z])
-
-    def ways(axis):
-        return {axis: step(axis, 1)}, {axis: step(axis, -1)}
-
-    def ring_sends(phase, u, p, r, a):
-        axis = UNITS[u][phase]
-        right, left_ = ways(axis)
-        far, near, back = (p[u].at[step(axis, by)] for by in (2, 1, -1))
-        send(("x", phase, u), far.at[0:2], r[u].at[0], right, ("s", phase, u))
-        send(("x", phase, u), far.at[2:4], r[u].at[1], left_, ("s", phase, u))
-        send(("a", phase, u), near.at[2:4], a[u].at[0, 2:4], right, ("s", phase, u))
-        send(("a", phase, u), back.at[0:2], a[u].at[1, 0:2], left_, ("s", phase, u))
-
-    def relay(phase, us, p, r, a):
-        for u in us:
-            axis = UNITS[u][phase]
-            right, left_ = ways(axis)
-            near, back = (p[u].at[step(axis, by)] for by in (1, -1))
-            arrived(("x", phase, u), r[u])
-            near[0:2] = (near[0:2].astype(F32) + r[u][0].astype(F32)).astype(BF16)
-            back[2:4] = (back[2:4].astype(F32) + r[u][1].astype(F32)).astype(BF16)
-            send(("a", phase, u), near.at[0:2], a[u].at[0, 0:2], right, ("s", phase, u))
-            send(("a", phase, u), back.at[2:4], a[u].at[1, 2:4], left_, ("s", phase, u))
-
-    def second(u, t):
-        return own[u].at[:, t] if u % 3 == 1 else own[u].at[t]
-
-    def second_sends(us):
-        for u in us:
-            arrived(("a", 1, u), ra[u])
-            total = part[u][at[UNITS[u][1]]].astype(F32) + (ra[u][0].astype(F32) + ra[u][1].astype(F32))
-            own[u][...] = total
-            if u % 3 == 1:
-                for z in range(4):
-                    part2[u][:, z] = total[z].astype(BF16)
-            else:
-                part2[u][...] = total.astype(BF16)
-            ring_sends(2, u, part2, rx2, ra2)
-
-    def third_sends(us):
-        for u in us:
-            arrived(("a", 2, u), ra2[u])
-            mine = second(u, at[UNITS[u][2]])
-            mine[...] += ra2[u][0].astype(F32) + ra2[u][1].astype(F32)
-            for slot, by in enumerate((2, 1, -1)):
-                part3[u][slot] = mine[step(UNITS[u][3], by)].astype(BF16)
-                send(("a", 3, u), part3[u].at[slot], ra3[u].at[slot],
-                     {UNITS[u][3]: step(UNITS[u][3], by)}, ("s", 3, u))
-
-    def last_sums(us):
-        for u in us:
-            arrived(("a", 3, u), ra3[u])
-            mine = second(u, at[UNITS[u][2]])[at[UNITS[u][3]]]
-            fin_ref[ic, :, GOFF[u]:GOFF[u] + UNITS[u][0]] = mine + (
-                ra3[u][0].astype(F32) + ra3[u][1].astype(F32) + ra3[u][2].astype(F32))
-
-    mark("firstA")
-    products_a()
-    for u in A:
-        ring_sends(1, u, part, rx, ra)
-    mark("mateB")
+    arrived("j1", jp.at[:, 384:768])
+    mark("firstA1")
+    products(1)
+    mark("secondA0")
+    second_sends(A0)
     arrived(("kvg",), kvgp)
     arrived(("jl",), jp.at[:, 768:1024])
     arrived(("rg",), rgp)
@@ -578,31 +593,36 @@
     products_b()
     for u in B:
         ring_sends(1, u, part, rx, ra)
+    mark("relayA1")
+    relay(1, A1, part, rx, ra)
+    mark("relay2A0")
+    relay(2, A0, part2, rx2, ra2)
     mark("tg")
     token_block()
-    mark("relayA")
-    relay(1, A, part, rx, ra)
-    mark("tg")
     token_block()
     token_block()
     mark("relayB")
     relay(1, B, part, rx, ra)
     mark("tg")
     token_block()
-    mark("secondA")
-    second_sends(A)
+    mark("thirdA0")
+    third_sends(A0)
+    mark("secondA1")
+    second_sends(A1)
     mark("secondB")
     second_sends(B)
-    mark("relay2A")
-    relay(2, A, part2, rx2, ra2)
+    mark("relay2A1")
+    relay(2, A1, part2, rx2, ra2)
     mark("relay2B")
     relay(2, B, part2, rx2, ra2)
-    mark("thirdA")
-    third_sends(A)
+    mark("thirdA1")
+    third_sends(A1)
     mark("thirdB")
     third_sends(B)
-    mark("lastA")
-    last_sums(A)
+    mark("lastA0")
+    last_sums(A0)
+    mark("lastA1")
+    last_sums(A1)
     send(("fin", 0), fin_ref.at[ic, :, 0:768], fin_ref.at[ic, :, 0:768], mate)
     mark("lastB")
     last_sums(B)
@@ -653,6 +673,7 @@
     mark("drain")
     for key, ref in owed:
         left(key, ref)
+    left("j0", jb.at[0, :, 0:384])
     left("g", gbuf.at[0:3, 0])
     left("gd", gbuf.at[:, 0])
     for kind in KINDS:
@@ -672,8 +693,8 @@
     assert len(recv_table) == NRECV and len(send_table) == NSEND, (len(recv_table), len(send_table))
 
 
-NRECV = 72
-NSEND = 40
+NRECV = 88
+NSEND = 50
 
 
 def scratch():
@@ -737,15 +758,15 @@
         return slice(lo, lo + 128)
 
     for n in range(4):
-        half, m = n // 2, n % 2
-        rope = rows(half, cols(512 + m * 128))
+        half, lo = n % 2, n // 2 * 384
+        rope = rows(half, cols(lo + 256))
         gq_ref[:, n * 384:(n + 1) * 384] = jnp.concatenate(
-            [rows(half, cols(m * 256)), rope[:, :64], rows(half, cols(m * 256 + 128)), rope[:, 64:]], 1)
-        gd_ref[:, n * 128:(n + 1) * 128] = rows(half, cols(768 + m * 256))
+            [rows(half, cols(lo)), rope[:, :64], rows(half, cols(lo + 128)), rope[:, 64:]], 1)
+        gd_ref[:, n * 128:(n + 1) * 128] = rows(n // 2, cols(768 + n % 2 * 256))
     tail = slice(GTOT - 128, GTOT)
     gd_ref[:, 512:576] = jnp.concatenate([rows(0, tail)[:, :32], rows(1, tail)[:, :32]], 1)
     for h in range(H):
-        half, j = h // 4, h % 4
+        half, j = h // 2 % 2, h // 4 * 2 + h % 2
         for u in range(2):
             block = fin_ref[half, j * 8:j * 8 + 8, cols(896 + u * 256)] * clip
             gu_ref[:, h * 256 + u * 128:h * 256 + u * 128 + 128] = jnp.where(first, block[0:4], block[4:8])

time: 101 us -> 97.1 us (0.961)
  Pallas kernels: 99.7 us -> 96.2 us
    pallas_call x1, Pallas kernels: 96.5 us -> 92.9 us  [per_device(): pl.pallas_call(mega, out_shape=(jax.ShapeDtypeStruct((2, 32, GTOT), F32),...]
where the time goes in v4:
time: 97.1 us; the launch traced here: 97 us
  Pallas kernels  96.2 us (99%)
    pallas_call x1, Pallas kernels, per_device(): pl.pallas_call(mega, out_shape=(jax.ShapeDtypeStruct((2, 32, GTOT), F32),...  92.9 us
    pallas_call x1, Pallas kernels, finish(): pl.pallas_call(last_step, out_shape=(jax.ShapeDtypeStruct((16, 1536), F32...  3.22 us

profile of v4, /device:TPU:1, one launch (start us, length us, event | category | flops | bytes accessed | tf_op | source)
XLA Modules:
  0.0 97.0 jit_solution(2281219881801114965)
XLA Ops:
  0.6 92.9 %shard_map.119 = (f32[2,32,1408]{2,1,0:T(8,128)}, f32[8,128]{1,0:T(8,128)}, bf16[512,2048]{1,0:T(8,128)(2,1)}) custom-call(bf16[512,2048]{1,0:T(8,128)(2,1)} %tokens_hbm.1, bf16[512,1024]{1,0:T(8,128)(2,1)} %dout_hbm.1, f32[512,128]{1,0:T(8,128)} %constant.4.clone.cos_hbm, f32[512,128]{1,0:T(8,128)} %constant.5.clone.sin_hbm, bf16[256,1536]{1,0:T(8,128)(2,1)} %wq_hbm.1, ...), custom_call_target="tpu_custom_call" | custom-call | tf_op jit(solution)/shard_map/pallas_call | solution.py:806
  93.6 3.2 %shard_map.120 = (f32[16,1536]{1,0:T(8,128)}, f32[16,576]{1,0:T(8,128)}, f32[4,2048]{1,0:T(4,128)}, f32[4]{0:T(128)}, bf16[512,2048]{1,0:T(8,128)(2,1)}) custom-call(f32[2,32,1408]{2,1,0:T(8,128)} %get-tuple-element.8.fin_hbm, f32[8,128]{1,0:T(8,128)} %get-tuple-element.9.clip_hbm, bf16[512,2048]{1,0:T(8,128)(2,1)} %get-tuple-element.10.tg_in), custom_call_target="tpu_custom_call" | custom-call | tf_op jit(solution)/shard_map/pallas_call | solution.py:785

commit v5 on v4

--- a/solution.py
+++ b/solution.py
@@ -28,8 +28,9 @@
 SUBS = ((0, 640), (640, 1408), (1408, 2176))
 SCALE = 1.0 / math.sqrt(DN + DR)
 AXES = ((AZ, AX, AY), (AX, AY, AZ), (AY, AZ, AX))
-UNITS = tuple((w,) + AXES[n % 3] for n, w in enumerate((128,) * 6 + (256, 256, 128)))
-GOFF = (0, 128, 256, 384, 512, 640, 768, 1024, 1280)
+GRP = (0, 1, 2, 0, 1, 2, 0, 1, 0, 1, 2)
+UNITS = tuple((128,) + AXES[g] for g in GRP)
+GOFF = tuple(128 * n for n in range(len(GRP)))
 GTOT = 1408
 F32 = jnp.float32
 BF16 = jnp.bfloat16
@@ -370,9 +371,9 @@
         ds = (probs * (dp - delta) * SCALE).astype(BF16)
         return probs.astype(BF16), ds
 
-    A0, A1, B = (0, 1, 2), (3, 4, 5), (6, 7, 8)
+    A0, A1, U, B = (0, 1, 2), (3, 4, 5), (6, 7), (8, 9, 10)
     def keep(u, z, cols, value):
-        g = u % 3
+        g = GRP[u]
         value = value.astype(BF16)
         if g == 0:
             part[u][z, :, :, :, cols] = value
@@ -402,16 +403,21 @@
             jnp.concatenate([jp[:, 768:1024], rgp[...]], 1)], 0)
         for z in range(4):
             both = nn(token_rows(z), right).reshape(4, 4, 32, 384)
-            for u in (6, 7):
-                keep(u, z, slice(0, 128), both[..., (u - 6) * 128:(u - 5) * 128])
-            keep(8, z, slice(0, 128), both[..., 256:] + gmat[z])
-        for u in (6, 7):
+            for u in (8, 9):
+                keep(u, z, slice(0, 128), both[..., (u - 8) * 128:(u - 7) * 128])
+            keep(10, z, slice(0, 128), both[..., 256:] + gmat[z])
+        for u in B:
+            ring_sends(1, u, part, rx, ra)
+
+    def products_u():
+        for u in U:
             up = nn(nrt[...], jnp.concatenate([kvg[ic, u - 6], kvgp[u - 6]], 0))
             up = up.reshape(64, 8, 512)
             up = jnp.concatenate([up[:, :, j * 128:(j + 1) * 128] for j in range(4)], 1)
             up = up.reshape(4, 4, 4, 32, 128)
             for z in range(4):
-                keep(u, z, slice(128, 256), up[z])
+                keep(u, z, slice(0, 128), up[z])
+            ring_sends(1, u, part, rx, ra)
 
     def ways(axis):
         return {axis: step(axis, 1)}, {axis: step(axis, -1)}
@@ -437,14 +443,14 @@
             send(("a", phase, u), back.at[2:4], a[u].at[1, 2:4], left_, ("s", phase, u))
 
     def second(u, t):
-        return own[u].at[:, t] if u % 3 == 1 else own[u].at[t]
+        return own[u].at[:, t] if GRP[u] == 1 else own[u].at[t]
 
     def second_sends(us):
         for u in us:
             arrived(("a", 1, u), ra[u])
             total = part[u][at[UNITS[u][1]]].astype(F32) + (ra[u][0].astype(F32) + ra[u][1].astype(F32))
             own[u][...] = total
-            if u % 3 == 1:
+            if GRP[u] == 1:
                 for z in range(4):
                     part2[u][:, z] = total[z].astype(BF16)
             else:
@@ -536,12 +542,14 @@
         @pl.when(n == 1)
         def _():
             send("j0", jb.at[other, :, 0:384], jp.at[:, 0:384], mate, "j0")
+            send("kv0", kvg.at[other, :, :, 0:256], kvgp.at[:, :, 0:256], mate, "kv0")
 
         return carry
 
     lax.fori_loop(0, 4, pair, 0)
     mark("post")
     send("j1", jb.at[other, :, 384:768], jp.at[:, 384:768], mate)
+    send("kv1", kvg.at[other, :, :, 256:512], kvgp.at[:, :, 256:512], mate)
     relay(1, A0, part, rx, ra)
 
     gterm = jnp.zeros((1, 512), F32)
@@ -560,7 +568,6 @@
     rgf[...] = rope.astype(BF16)
     rg[0] = jnp.where(lane < 32, rope, 0.0).astype(BF16)
     rg[1] = jnp.where(lane < 32, pltpu.roll(rope, 96, 1), 0.0).astype(BF16)
-    send(("kvg",), kvg.at[other], kvgp, mate)
     send(("jl",), jb.at[other, :, 768:1024], jp.at[:, 768:1024], mate)
     send(("rg",), rg.at[other], rgp, mate)
     column = jnp.broadcast_to(gterm, (128, 512)).T
@@ -581,18 +588,21 @@
 
     mark("waitmate")
     arrived(("nrt",), nrt.at[:, 512:1024])
+    arrived("kv0", kvgp.at[:, :, 0:256])
+    arrived("kv1", kvgp.at[:, :, 256:512])
+    mark("firstU")
+    products_u()
     arrived("j1", jp.at[:, 384:768])
     mark("firstA1")
     products(1)
     mark("secondA0")
     second_sends(A0)
-    arrived(("kvg",), kvgp)
     arrived(("jl",), jp.at[:, 768:1024])
     arrived(("rg",), rgp)
     mark("productsB")
     products_b()
-    for u in B:
-        ring_sends(1, u, part, rx, ra)
+    mark("relayU")
+    relay(1, U, part, rx, ra)
     mark("relayA1")
     relay(1, A1, part, rx, ra)
     mark("relay2A0")
@@ -600,36 +610,41 @@
     mark("tg")
     token_block()
     token_block()
-    token_block()
     mark("relayB")
     relay(1, B, part, rx, ra)
     mark("tg")
     token_block()
+    token_block()
     mark("thirdA0")
     third_sends(A0)
+    mark("secondU")
+    second_sends(U)
     mark("secondA1")
     second_sends(A1)
     mark("secondB")
     second_sends(B)
+    mark("relay2U")
+    relay(2, U, part2, rx2, ra2)
     mark("relay2A1")
     relay(2, A1, part2, rx2, ra2)
     mark("relay2B")
     relay(2, B, part2, rx2, ra2)
     mark("thirdA1")
+    third_sends(U)
     third_sends(A1)
     mark("thirdB")
     third_sends(B)
-    mark("lastA0")
+    mark("lastA")
     last_sums(A0)
-    mark("lastA1")
+    last_sums(U)
     last_sums(A1)
-    send(("fin", 0), fin_ref.at[ic, :, 0:768], fin_ref.at[ic, :, 0:768], mate)
+    send(("fin", 0), fin_ref.at[ic, :, 0:1024], fin_ref.at[ic, :, 0:1024], mate)
     mark("lastB")
     last_sums(B)
-    send(("fin", 1), fin_ref.at[ic, :, 768:GTOT], fin_ref.at[ic, :, 768:GTOT], mate)
+    send(("fin", 1), fin_ref.at[ic, :, 1024:GTOT], fin_ref.at[ic, :, 1024:GTOT], mate)
     mark("fin")
-    arrived(("fin", 0), fin_ref.at[other, :, 0:768])
-    arrived(("fin", 1), fin_ref.at[other, :, 768:GTOT])
+    arrived(("fin", 0), fin_ref.at[other, :, 0:1024])
+    arrived(("fin", 1), fin_ref.at[other, :, 1024:GTOT])
 
     both = fin_ref[...]
     tail = GTOT - 128
@@ -674,6 +689,7 @@
     for key, ref in owed:
         left(key, ref)
     left("j0", jb.at[0, :, 0:384])
+    left("kv0", kvg.at[0, :, :, 0:256])
     left("g", gbuf.at[0:3, 0])
     left("gd", gbuf.at[:, 0])
     for kind in KINDS:
@@ -693,8 +709,8 @@
     assert len(recv_table) == NRECV and len(send_table) == NSEND, (len(recv_table), len(send_table))
 
 
-NRECV = 88
-NSEND = 50
+NRECV = 99
+NSEND = 57
 
 
 def scratch():
@@ -762,13 +778,13 @@
         rope = rows(half, cols(lo + 256))
         gq_ref[:, n * 384:(n + 1) * 384] = jnp.concatenate(
             [rows(half, cols(lo)), rope[:, :64], rows(half, cols(lo + 128)), rope[:, 64:]], 1)
-        gd_ref[:, n * 128:(n + 1) * 128] = rows(n // 2, cols(768 + n % 2 * 256))
+        gd_ref[:, n * 128:(n + 1) * 128] = rows(n // 2, cols(1024 + n % 2 * 128))
     tail = slice(GTOT - 128, GTOT)
     gd_ref[:, 512:576] = jnp.concatenate([rows(0, tail)[:, :32], rows(1, tail)[:, :32]], 1)
     for h in range(H):
         half, j = h // 2 % 2, h // 4 * 2 + h % 2
         for u in range(2):
-            block = fin_ref[half, j * 8:j * 8 + 8, cols(896 + u * 256)] * clip
+            block = fin_ref[half, j * 8:j * 8 + 8, cols(768 + u * 128)] * clip
             gu_ref[:, h * 256 + u * 128:h * 256 + u * 128 + 128] = jnp.where(first, block[0:4], block[4:8])
     gain = (fin_ref[0, 0:8, tail] + fin_ref[1, 0:8, tail]) * clip
     gain = jnp.where(first, gain[0:4], gain[4:8])

time: 97.1 us -> 95.6 us (0.985)
  Pallas kernels: 96.2 us -> 94.7 us
    pallas_call x1, Pallas kernels: 92.9 us -> 91.5 us  [per_device(): pl.pallas_call(mega, out_shape=(jax.ShapeDtypeStruct((2, 32, GTOT), F32),...]
where the time goes in v5:
time: 95.6 us; the launch traced here: 95.5 us
  Pallas kernels  94.7 us (99%)
    pallas_call x1, Pallas kernels, per_device(): pl.pallas_call(mega, out_shape=(jax.ShapeDtypeStruct((2, 32, GTOT), F32),...  91.5 us
    pallas_call x1, Pallas kernels, finish(): pl.pallas_call(last_step, out_shape=(jax.ShapeDtypeStruct((16, 1536), F32...  3.22 us

profile of v5, /device:TPU:1, one launch (start us, length us, event | category | flops | bytes accessed | tf_op | source)
XLA Modules:
  0.0 95.5 jit_solution(8713937359383535614)
XLA Ops:
  0.6 91.5 %shard_map.119 = (f32[2,32,1408]{2,1,0:T(8,128)}, f32[8,128]{1,0:T(8,128)}, bf16[512,2048]{1,0:T(8,128)(2,1)}) custom-call(bf16[512,2048]{1,0:T(8,128)(2,1)} %tokens_hbm.1, bf16[512,1024]{1,0:T(8,128)(2,1)} %dout_hbm.1, f32[512,128]{1,0:T(8,128)} %constant.4.clone.cos_hbm, f32[512,128]{1,0:T(8,128)} %constant.5.clone.sin_hbm, bf16[256,1536]{1,0:T(8,128)(2,1)} %wq_hbm.1, ...), custom_call_target="tpu_custom_call" | custom-call | tf_op jit(solution)/shard_map/pallas_call | solution.py:822
  92.1 3.2 %shard_map.120 = (f32[16,1536]{1,0:T(8,128)}, f32[16,576]{1,0:T(8,128)}, f32[4,2048]{1,0:T(4,128)}, f32[4]{0:T(128)}, bf16[512,2048]{1,0:T(8,128)(2,1)}) custom-call(f32[2,32,1408]{2,1,0:T(8,128)} %get-tuple-element.8.fin_hbm, f32[8,128]{1,0:T(8,128)} %get-tuple-element.9.clip_hbm, bf16[512,2048]{1,0:T(8,128)(2,1)} %get-tuple-element.10.tg_in), custom_call_target="tpu_custom_call" | custom-call | tf_op jit(solution)/shard_map/pallas_call | solution.py:801

commit v6 on v5

--- a/solution.py
+++ b/solution.py
@@ -59,9 +59,9 @@
 
 def mega(
     tokens_hbm, dout_hbm, cos_hbm, sin_hbm, wq_hbm, wd_hbm, wu_hbm, gain_hbm,
-    fin_ref, clip_ref, tg_hbm,
+    fin_ref, clip_ref, tg_ref,
     tokens, dout, cosr, sinr, wbuf, ubuf, gbuf, tokt, acc, qrope, qnope, nrm, nrt, ng, krp, dkr,
-    jb, jp, kvg, kvgp, rg, rgp, rgf, invr, gmat, tgb, nbuf, wq_ref, wd_ref, gain_ref, lsem, ssem, rsem, *rest,
+    jb, jp, kvg, kvgp, rg, rgp, rgf, invr, gmat, nbuf, wq_ref, wd_ref, gain_ref, lsem, ssem, rsem, *rest,
 ):
     nu = len(UNITS)
     part, own, rx, ra, part2, rx2, ra2, part3, ra3 = (rest[n * nu:(n + 1) * nu] for n in range(9))
@@ -581,10 +581,8 @@
         w = wbuf[n].reshape(512, WCOL)
         cols = [jb[0, :, 768:], jb[1, :, 768:], rgf[...]]
         cols += [jb[m % 2, :, m // 2 * 384:m // 2 * 384 + 384] for m in range(4)]
-        tgb[n] = nt(jnp.concatenate(cols, 1), w).astype(BF16)
-        d = pltpu.make_async_copy(tgb.at[n], tg_hbm.at[:, n * 512:(n + 1) * 512], lsem.at[9])
-        d.start()
-        tgd.append(d)
+        tg_ref[:, n * 512:(n + 1) * 512] = nt(jnp.concatenate(cols, 1), w).astype(BF16)
+        tgd.append(n)
 
     mark("waitmate")
     arrived(("nrt",), nrt.at[:, 512:1024])
@@ -704,7 +702,6 @@
         left(("s", 1, u), part[u].at[0:3])
         left(("s", 2, u), part2[u].at[0:3])
         left(("s", 3, u), part3[u])
-    pltpu.make_async_copy(tgb, tgb, lsem.at[9]).wait()
     mark(None)
     assert len(recv_table) == NRECV and len(send_table) == NSEND, (len(recv_table), len(send_table))
 
@@ -724,7 +721,7 @@
         v((512, 512), F32), v((2, 512, 128), BF16), v((512, 128), F32),
         v((2, 512, 1024), BF16), v((512, 1024), BF16), v((2, 2, 512, 512), BF16), v((2, 512, 512), BF16),
         v((2, 512, 128), BF16), v((512, 128), BF16), v((512, 128), BF16), v((512, 128), F32),
-        v((4, 4, 4, 32, 128), F32), v((4, 512, 512), BF16), v((4, 4, 8, 128), F32),
+        v((4, 4, 4, 32, 128), F32), v((4, 4, 8, 128), F32),
         v((256, 1536), BF16), v((576, 256), BF16), v((1, 64), BF16),
         dma((10,)), dma((NSEND,)), dma((NRECV,)),
     ]
@@ -741,29 +738,10 @@
     return shapes
 
 
-def last_step(fin_hbm, clip_hbm, tg_in, gq_ref, gd_ref, gu_ref, gg_ref, tg_out,
-              fin_ref, clip_ref, stage, isem, osem):
+def last_step(fin_ref, clip_ref, tg_ref, gq_ref, gd_ref, gu_ref, gg_ref, tg_hbm, sem):
+    whole = pltpu.make_async_copy(tg_ref, tg_hbm, sem)
+    whole.start()
     ic = lax.axis_index(AC)
-    first_reads = []
-    for n, (src, dst) in enumerate(((fin_hbm, fin_ref), (clip_hbm, clip_ref))):
-        d = pltpu.make_async_copy(src, dst, isem.at[4 + n])
-        d.start()
-        first_reads.append(d)
-    reads = []
-    for n in range(4):
-        rows = slice(n * 128, (n + 1) * 128)
-        d = pltpu.make_async_copy(tg_in.at[rows], stage.at[n], isem.at[n])
-        d.start()
-        reads.append(d)
-    writes = []
-    for n in range(4):
-        rows_n = slice(n * 128, (n + 1) * 128)
-        reads[n].wait()
-        d = pltpu.make_async_copy(stage.at[n], tg_out.at[rows_n], osem.at[n])
-        d.start()
-        writes.append(d)
-    for d in first_reads:
-        d.wait()
     clip = clip_ref[0:1, 0:1]
     first = ic == 0
 
@@ -791,14 +769,12 @@
     spread = (lax.broadcasted_iota(jnp.int32, (4, 128), 0)
               == lax.broadcasted_iota(jnp.int32, (4, 128), 1))
     gg_ref[...] = jnp.sum(jnp.where(spread, gain[:, 32:33], 0.0), axis=0)[0:4]
-    for d in writes:
-        d.wait()
+    whole.wait()
 
 
 def finish(fin, clip, token_grad):
     vm = pl.BlockSpec(memory_space=pltpu.VMEM)
-    anyspace = pl.BlockSpec(memory_space=pl.ANY)
-    return pl.pallas_call(
+    return tuple(pl.pallas_call(
         last_step,
         out_shape=(
             jax.ShapeDtypeStruct((16, 1536), F32),
@@ -807,12 +783,12 @@
             jax.ShapeDtypeStruct((4,), F32),
             jax.ShapeDtypeStruct((SEQ, D), BF16),
         ),
-        in_specs=[anyspace] * 3,
-        out_specs=(vm, vm, vm, vm, anyspace),
-        scratch_shapes=[
-            pltpu.VMEM((2, 32, GTOT), F32), pltpu.VMEM((8, 128), F32),
-            pltpu.VMEM((4, 128, D), BF16), pltpu.SemaphoreType.DMA((6,)), pltpu.SemaphoreType.DMA((4,))],
-    )(fin, clip, token_grad)
+        in_specs=[vm, vm, vm],
+        out_specs=(vm, vm, vm, vm, pl.BlockSpec(memory_space=pl.ANY)),
+        scratch_shapes=[pltpu.SemaphoreType.DMA],
+        compiler_params=pltpu.CompilerParams(vmem_limit_bytes=16 * 1024 * 1024),
+        cost_estimate=pl.CostEstimate(flops=4000000, bytes_accessed=800000, transcendentals=0),
+    )(fin, clip, token_grad))
 
 
 def per_device(tokens, d_out, w_query, w_down, w_up, latent_gain):
@@ -822,15 +798,15 @@
     fin, clip, token_grad = pl.pallas_call(
         mega,
         out_shape=(
-            jax.ShapeDtypeStruct((2, 32, GTOT), F32),
-            jax.ShapeDtypeStruct((8, 128), F32),
-            jax.ShapeDtypeStruct((SEQ, D), BF16),
+            pltpu.VMEM((2, 32, GTOT), F32),
+            pltpu.VMEM((8, 128), F32),
+            pltpu.VMEM((SEQ, D), BF16),
         ),
         in_specs=[anyspace] * 8,
-        out_specs=(vm, vm, anyspace),
+        out_specs=(vm, vm, vm),
         scratch_shapes=scratch(),
         compiler_params=pltpu.CompilerParams(
-            collective_id=0, has_side_effects=True, vmem_limit_bytes=67043328),
+            collective_id=0, has_side_effects=True, vmem_limit_bytes=58 * 1024 * 1024),
     )(tokens, d_out, jnp.asarray(cosine), jnp.asarray(sine), w_query, w_down.T, w_up,
       latent_gain.reshape(1, 64))
     return finish(fin, clip, token_grad)

time: 95.6 us -> 93.5 us (0.978)
  Pallas kernels: 94.7 us -> 92.6 us
    pallas_call x1, Pallas kernels: 3.22 us -> 2 us  [finish(): pl.pallas_call(last_step, out_shape=(jax.ShapeDtypeStruct((16, 1536), F32...]
where the time goes in v6:
time: 93.5 us; the launch traced here: 93.4 us
  Pallas kernels  92.6 us (99%)
    pallas_call x1, Pallas kernels, per_device(): pl.pallas_call(mega, out_shape=(pltpu.VMEM((2, 32, GTOT), F32), pltpu.VME...  90.6 us
    pallas_call x1, Pallas kernels, finish(): pl.pallas_call(last_step, out_shape=(jax.ShapeDtypeStruct((16, 1536), F32...  2 us

profile of v6, /device:TPU:1, one launch (start us, length us, event | category | flops | bytes accessed | tf_op | source)
XLA Modules:
  0.0 93.4 jit_solution(15793581868473020217)
XLA Ops:
  0.6 90.6 %shard_map.119 = (f32[2,32,1408]{2,1,0:T(8,128)S(1)}, f32[8,128]{1,0:T(8,128)S(1)}, bf16[512,2048]{1,0:T(8,128)(2,1)S(1)}) custom-call(bf16[512,2048]{1,0:T(8,128)(2,1)} %tokens_hbm.1, bf16[512,1024]{1,0:T(8,128)(2,1)} %dout_hbm.1, f32[512,128]{1,0:T(8,128)} %constant.4.clone.cos_hbm, f32[512,128]{1,0:T(8,128)} %constant.5.clone.sin_hbm, ...), custom_call_target="tpu_custom_call" | custom-call | tf_op jit(solution)/shard_map/pallas_call | solution.py:798
  91.2 2.0 %shard_map.120 = (f32[16,1536]{1,0:T(8,128)}, f32[16,576]{1,0:T(8,128)}, f32[4,2048]{1,0:T(4,128)}, f32[4]{0:T(128)}, bf16[512,2048]{1,0:T(8,128)(2,1)}) custom-call(f32[2,32,1408]{2,1,0:T(8,128)S(1)} %get-tuple-element.8.fin_ref, f32[8,128]{1,0:T(8,128)S(1)} %get-tuple-element.9.clip_ref, bf16[512,2048]{1,0:T(8,128)(2,1)S(1)} %get-tuple-element.10.tg_ref), custom_call_target="tpu_custom_call" | custom-call | flops 4000000 | bytes 800000 | tf_op jit(solution)/shard_map/pallas_call | solution.py:777
